TPU v7x, 128 devices: a whole 4x4x4 slice. The times are simulated.
128 devices in a mesh: row: 8 (over x, core), col: 16 (over y, z).
Axes of the slice: x: 4, y: 4, z: 4, core: 2. Of those that a mesh axis runs over, the one named last changes fastest.
Arguments:
- matrix: float32 [6144, 6, 8192], P('row', None, 'col'), may hold values from -6 to 6
- factor: float32 [6, 8192, 2048], P(None, 'col', 'row'), as said below
Outputs:
- updated: float32 [6144, 6, 8192], P('row', None, 'col')
- solved: float32 [6144, 2048], P('row')
Inputs may be any that keep to these rules, and one draw needn't show every extreme that they name: factor is lower trapezoidal: zero wherever the column index exceeds the row index; its diagonal entries lie in 1 to 2.
All inputs are finite; a program needn't handle non-finite values.
Results may differ from a plain program's by a relative error of at most 0.00013.
Values sent between devices are 32-bit elements; how exact they have to be, the bound alone decides.
No kernel may reach another device: no remote copies, remote signals or barrier semaphores. Data moves between devices by JAX's collectives and lax.ppermute only.
A program may use at most 256 MiB of HBM per device.

v0:
```python
import jax
import jax.numpy as jnp
from jax import lax
from jax.sharding import Mesh
from jax.sharding import PartitionSpec as P

P_SIZE = 4
ROW = ("row_0", "row_1")


def from_root(value, axis, source):
    kept = jnp.where(lax.axis_index(axis) == source, value, 0).astype(value.dtype)
    return lax.psum(kept, axis)


def edges_of(length, count):
    unit = 8 if length >= 8 * count else 1
    return [length // unit * k // count * unit for k in range(1, count)]


def stacked_from(shard, axes, sequence):
    pieces = shard
    for k in sequence:
        pieces = lax.all_gather(pieces, axes[k])
    done = sequence[::-1]
    back = [done.index(k) for k in range(len(axes))]
    pieces = pieces.transpose(*back, *range(len(axes), pieces.ndim))
    return pieces.reshape(-1, *shard.shape)


def laid_out(pieces, dim):
    dims = list(pieces.shape[1:])
    dims[dim] *= pieces.shape[0]
    return jnp.moveaxis(pieces, 0, dim).reshape(dims)


def gather_all_axes(shard, axes, dim):
    cut = max(range(max(1, shard.ndim - 1)), key=lambda d: shard.shape[d])
    count, finished = (len(axes), [])
    for first, share in enumerate(jnp.split(shard, edges_of(shard.shape[cut], count), axis=cut)):
        if share.size:
            sequence = [(first - k) % count for k in range(count)]
            finished.append(stacked_from(share, axes, sequence))
    return laid_out(jnp.concatenate(finished, axis=cut + 1), dim)


def local(matrix, factor):
    col_count = lax.axis_size("col")
    col_index = lax.axis_index("col")
    nlocal = matrix.shape[1]
    block_width = matrix.shape[2]
    block_ids = jnp.arange(nlocal, dtype=jnp.int32) * col_count + col_index
    unit_block = jnp.eye(block_width, dtype=jnp.float32)
    panels = []
    head_count = (P_SIZE - 1) // col_count + 1
    head_tiles = gather_all_axes(factor[:head_count], ROW, 2)
    for step in range(P_SIZE):
        local_block = step // col_count
        right_side = matrix[:, local_block, :]
        if step > 0:
            earlier = jnp.concatenate(panels, axis=1)
            right_side = right_side - jnp.dot(
                earlier,
                head_tiles[local_block, :, : step * block_width].T,
                precision=lax.Precision.HIGHEST,
                preferred_element_type=jnp.float32,
            )
        diag_tile = head_tiles[local_block, :, step * block_width : (step + 1) * block_width]
        root_col = step % col_count
        guarded = jnp.where(col_index == root_col, diag_tile, unit_block)
        solved_block = lax.linalg.triangular_solve(
            guarded, right_side, left_side=False, lower=True, transpose_a=True
        )
        panels.append(from_root(solved_block, "col", root_col))
    solved = jnp.concatenate(panels, axis=1)
    piece = lax.all_gather(factor, ROW, axis=2, tiled=True)
    piece_width = piece.shape[2]
    panel_of = jnp.arange(piece_width, dtype=jnp.int32) // block_width
    active = panel_of[None, :] < block_ids[:, None]
    masked = jnp.where(active[:, None, :], piece, jnp.zeros((), piece.dtype))
    running = jnp.einsum("ms,lts->mlt", solved, masked, precision=lax.Precision.HIGHEST)
    updated = matrix - running
    return (updated, solved)


def solution(mesh):
    finer = Mesh(mesh.devices.reshape(4, 2, mesh.shape["col"]), ("row_0", "row_1", "col"))
    return jax.shard_map(
        local,
        mesh=finer,
        in_specs=(P(ROW, None, "col"), P(None, "col", ROW)),
        out_specs=(P(ROW, None, "col"), P(ROW, None)),
        check_vma=False,
    )
```

profile of v0, /device:TPU:1, one launch (start us, length us, event | category | flops | bytes accessed | tf_op | source)
XLA Modules:
  0.0 736.7 jit_solution(461420219002925032)
XLA Ops:
  8.0 1.8 fusion.112
  9.9 3.3 all-gather.2
  13.3 23.0 %all-gather.11.cloned.1.call-done = f32[4,256,256]{2,1,0:T(8,128)} async-done(((f32[1,256,256]{2,1,0:T(8,128)}), f32[4,256,256]{2,1,0:T(8,128)}) %all-gather.11.cloned.1.call-update) | async-done | bytes 1048592 | tf_op jit(solution)/shard_map/all_gather | solution.py:24
  36.4 2.7 slice_bitcast_fusion.4
  39.0 31.9 %all-gather.15.cloned.1.call-done = f32[8,256,256]{2,1,0:T(8,128)} async-done(((f32[2,256,256]{2,1,0:T(8,128)}), f32[8,256,256]{2,1,0:T(8,128)}) %all-gather.15.cloned.1.call-update) | async-done | bytes 2097168 | tf_op jit(solution)/shard_map/all_gather | solution.py:24
  71.0 1.9 copy.12
  72.9 13.7 %all-gather.13.cloned.1.call-done = f32[8,256,256]{2,1,0:T(8,128)} async-done(((f32[4,256,256]{2,1,0:T(8,128)}), f32[8,256,256]{2,1,0:T(8,128)}) %all-gather.13.cloned.1.call-update) | async-done | bytes 2097168 | tf_op jit(solution)/shard_map/all_gather | solution.py:24
  86.6 2.9 copy.11
  89.5 2.1 pad_maximum_fusion
  91.6 1.9 fusion.49
  94.6 11.7 %while.8 = (s32[]{:T(128)}, f32[512,512]{0,1:T(8,128)}, s32[4,2]{0,1:T(2,128)S(1)}, f32[4,128,128]{2,1,0:T(8,128)S(1)}, s32[]{:T(128)}) while((s32[]{:T(128)}, f32[512,512]{0,1:T(8,128)}, s32[4,2]{0,1:T(2,128)S(1)}, f32[4,128,128]{2,1,0:T(8,128)S(1)}, s32[]{:T(128)}) %tuple.78), condition=%wide.while_cond, body=%wide.while_body.sunk | while | flops 2 | bytes 393321 | solution.py:71
  95.2 2.2 dynamic-slice.22
  98.1 2.2 dynamic-slice.22
  101.0 2.2 dynamic-slice.22
  104.0 2.1 dynamic-slice.22
  106.2 39.3 %custom-call.6 = f32[4,128,128]{1,2,0:T(8,128)S(1)} custom-call(f32[4,128,128]{2,1,0:T(8,128)S(1)} %get-tuple-element.29), custom_call_target="InvertDiagBlocksLowerTriangular" | custom-call | tf_op jit(solution)/shard_map/triangular_solve/custom-call.1 | solution.py:71
  148.3 2.3 convolution_subtract_fusion.12
  151.1 3.1 convolution_subtract_fusion.7
  156.3 11.7 %while.9 = (s32[]{:T(128)}, f32[512,512]{0,1:T(8,128)}, s32[4,2]{0,1:T(2,128)S(1)}, f32[4,128,128]{2,1,0:T(8,128)S(1)}, s32[]{:T(128)}) while((s32[]{:T(128)}, f32[512,512]{0,1:T(8,128)}, s32[4,2]{0,1:T(2,128)S(1)}, f32[4,128,128]{2,1,0:T(8,128)S(1)}, s32[]{:T(128)}) %tuple.106), condition=%wide.while_cond.clone, body=%wide.while_body.clone.sunk | while | flops 2 | bytes 393321 | solution.py:71
  156.9 2.2 dynamic-slice.24
  159.9 2.2 dynamic-slice.24
  162.9 2.2 dynamic-slice.24
  165.8 2.1 dynamic-slice.24
  168.1 39.3 %custom-call.7 = f32[4,128,128]{1,2,0:T(8,128)S(1)} custom-call(f32[4,128,128]{2,1,0:T(8,128)S(1)} %get-tuple-element.30), custom_call_target="InvertDiagBlocksLowerTriangular" | custom-call | tf_op jit(solution)/shard_map/triangular_solve/custom-call.1 | solution.py:71
  207.4 37.6 %all-reduce.5.cloned.1.call-done = f32[768,512]{0,1:T(8,128)} async-done(((f32[768,512]{0,1:T(8,128)}), f32[768,512]{0,1:T(8,128)}) %all-reduce.5.cloned.1.call-update) | async-done | bytes 1572880 | tf_op jit(solution)/shard_map/psum | solution.py:13
  244.9 4.9 convolution_subtract_fusion
  252.6 2.3 convolution_subtract_fusion.11
  255.4 3.1 convolution_subtract_fusion.5
  260.4 8.8 %while.10 = (s32[]{:T(128)}, f32[512,512]{0,1:T(8,128)S(1)}, s32[4,2]{0,1:T(2,128)S(1)}, f32[4,128,128]{2,1,0:T(8,128)S(1)}, s32[]{:T(128)}) while((s32[]{:T(128)}, f32[512,512]{0,1:T(8,128)S(1)}, s32[4,2]{0,1:T(2,128)S(1)}, f32[4,128,128]{2,1,0:T(8,128)S(1)}, s32[]{:T(128)}) %tuple.107), condition=%wide.while_cond.clone.1, body=%wide.while_body.clone.1.sunk | while | flops 2 | bytes 393321 | solution.py:71
  269.2 39.8 %custom-call.8 = f32[4,128,128]{1,2,0:T(8,128)S(1)} custom-call(f32[4,128,128]{2,1,0:T(8,128)S(1)} %get-tuple-element.31), custom_call_target="InvertDiagBlocksLowerTriangular" | custom-call | tf_op jit(solution)/shard_map/triangular_solve/custom-call.1 | solution.py:71
  309.0 40.3 %all-reduce.7.cloned.1.call-done = f32[768,512]{0,1:T(8,128)} async-done(((f32[768,512]{0,1:T(8,128)}), f32[768,512]{0,1:T(8,128)}) %all-reduce.7.cloned.1.call-update) | async-done | bytes 1572880 | tf_op jit(solution)/shard_map/psum | solution.py:13
  349.3 7.6 %fusion.20 = f32[768,512]{1,0:T(8,128)S(1)} fusion(f32[1,512,2048]{1,2,0:T(8,128)} %bitcast.160, f32[768,512]{0,1:T(8,128)} %all-reduce.7.cloned.1.call-done, f32[768,512]{0,1:T(8,128)S(1)} %copy-done.1, f32[768,6,512]{2,0,1:T(8,128)} %param.4), kind=kOutput, calls=%fused_computation.36 | convolution fusion | flops 4833017856 | bytes 8388608 | tf_op jit(solution)/shard_map/dot_general | solution.py:62
  360.7 2.1 convolution_subtract_fusion.3
  364.7 12.2 %while.11 = (s32[]{:T(128)}, f32[512,512]{0,1:T(8,128)}, s32[4,2]{0,1:T(2,128)S(1)}, f32[4,128,128]{2,1,0:T(8,128)S(1)}, s32[]{:T(128)}) while((s32[]{:T(128)}, f32[512,512]{0,1:T(8,128)}, s32[4,2]{0,1:T(2,128)S(1)}, f32[4,128,128]{2,1,0:T(8,128)S(1)}, s32[]{:T(128)}) %tuple.108), condition=%wide.while_cond.clone.2, body=%wide.while_body.clone.2.sunk | while | flops 2 | bytes 393321 | solution.py:71
  365.6 2.2 dynamic-slice.28
  368.6 2.2 dynamic-slice.28
  371.7 2.2 dynamic-slice.28
  374.7 2.2 dynamic-slice.28
  377.0 39.9 %custom-call.9 = f32[4,128,128]{1,2,0:T(8,128)} custom-call(f32[4,128,128]{2,1,0:T(8,128)S(1)} %get-tuple-element.32), custom_call_target="InvertDiagBlocksLowerTriangular" | custom-call | tf_op jit(solution)/shard_map/triangular_solve/custom-call.1 | solution.py:71
  416.9 36.6 %all-reduce.9.cloned.1.call-done = f32[768,512]{0,1:T(8,128)} async-done(((f32[768,512]{0,1:T(8,128)}), f32[768,512]{0,1:T(8,128)}) %all-reduce.9.cloned.1.call-update) | async-done | bytes 1572880 | tf_op jit(solution)/shard_map/psum | solution.py:13
  453.5 17.7 %fusion.23 = f32[768,512]{1,0:T(8,128)S(1)} fusion(f32[1,512,2048]{1,2,0:T(8,128)} %bitcast.161, f32[768,512]{0,1:T(8,128)} %all-reduce.9.cloned.1.call-done, f32[768,512]{0,1:T(8,128)S(1)} %copy-done.2, f32[768,512]{0,1:T(8,128)S(1)} %copy-done.1, f32[768,6,512]{2,0,1:T(8,128)} %param.4), kind=kOutput, calls=%fused_computation.38 | convolution fusion | flops 7250509824 | bytes 11010048 | tf_op jit(solution)/shard_map/dot_general | solution.py:62
  473.9 2.3 convolution_subtract_fusion.9
  476.8 3.1 convolution_subtract_fusion.1
  487.0 83.3 %all-reduce.11.cloned.1.call-done = f32[768,512]{0,1:T(8,128)} async-done(((f32[768,512]{0,1:T(8,128)}), f32[768,512]{0,1:T(8,128)}) %all-reduce.11.cloned.1.call-update) | async-done | bytes 1572880 | tf_op jit(solution)/shard_map/psum | solution.py:13
  570.3 2.7 constant_dynamic-update-slice_fusion
  572.9 6.6 copy.18
  579.5 25.7 %all-gather.9.cloned.1.call-done = f32[6,512,2048]{2,1,0:T(8,128)} async-done(((f32[6,512,256]{2,1,0:T(8,128)}), f32[6,512,2048]{2,1,0:T(8,128)}) %all-gather.9.cloned.1.call-update) | async-done | bytes 25165840 | tf_op jit(solution)/shard_map/all_gather | solution.py:76
  605.2 123.8 %fusion.11 = f32[768,6,512]{2,0,1:T(8,128)} fusion(f32[768,6,512]{2,0,1:T(8,128)} %param.4, f32[6,512,2048]{2,1,0:T(8,128)} %all-gather.9.cloned.1.call-done, pred[6,2048]{1,0:T(8,128)(4,1)S(1)} %broadcast_compare_fusion, f32[768,2048]{0,1:T(8,128)} %constant_dynamic-update-slice_fusion), kind=kOutput, calls=%fused_computation.20 | convolution fusion | flops 57990709248 | bytes 50343936 | tf_op jit(solution)/shard_map/ms,lts->mlt/dot_general | solution.py:81
  (133 shorter events, 45.0 us)
Async XLA Ops:
  8.0 28.3 %all-gather.11.cloned.1.call-start = ((), (), s32[]{:S(2)}) async-start(), calls=%async_computation.5 | async-start | bytes 1310720 | tf_op jit(solution)/shard_map/all_gather | solution.py:24
  9.8 61.1 %all-gather.15.cloned.1.call-start = ((), (), s32[]{:S(2)}) async-start(), calls=%async_computation.7 | async-start | bytes 2621440 | tf_op jit(solution)/shard_map/all_gather | solution.py:24
  13.2 73.3 %all-gather.13.cloned.1.call-start = ((), (), s32[]{:S(2)}) async-start(), calls=%async_computation.6 | async-start | bytes 3145728 | tf_op jit(solution)/shard_map/all_gather | solution.py:24
  36.3 208.7 %all-reduce.5.cloned.1.call-start = ((), (), s32[]{:S(2)}) async-start(), calls=%async_computation | async-start | bytes 3145728 | tf_op jit(solution)/shard_map/psum | solution.py:13
  91.6 3.0 copy-start
  91.6 54.0 %copy-start.3 = (f32[768,512]{1,0:T(8,128)S(1)}, f32[768,512]{1,0:T(8,128)}, u32[]{:S(2)}) copy-start(f32[768,512]{1,0:T(8,128)} %slice_bitcast_fusion.4) | copy-start | bytes 4718596
  156.0 193.2 %all-reduce.7.cloned.1.call-start = ((), (), s32[]{:S(2)}) async-start(), calls=%async_computation.1 | async-start | bytes 3145728 | tf_op jit(solution)/shard_map/psum | solution.py:13
  260.3 89.0 %copy-start.1 = (f32[768,512]{0,1:T(8,128)S(1)}, f32[768,512]{0,1:T(8,128)}, u32[]{:S(2)}) copy-start(f32[768,512]{0,1:T(8,128)} %all-reduce.5.cloned.1.call-done) | copy-start | bytes 4718596
  260.3 193.2 %all-reduce.9.cloned.1.call-start = ((), (), s32[]{:S(2)}) async-start(), calls=%async_computation.2 | async-start | bytes 3145728 | tf_op jit(solution)/shard_map/psum | solution.py:13
  364.6 88.9 %copy-start.2 = (f32[768,512]{0,1:T(8,128)S(1)}, f32[768,512]{0,1:T(8,128)}, u32[]{:S(2)}) copy-start(f32[768,512]{0,1:T(8,128)} %all-reduce.7.cloned.1.call-done) | copy-start | bytes 4718596
  364.7 205.6 %all-reduce.11.cloned.1.call-start = ((), (), s32[]{:S(2)}) async-start(), calls=%async_computation.3 | async-start | bytes 3145728 | tf_op jit(solution)/shard_map/psum | solution.py:13
  416.9 54.3 %copy-start.5 = (f32[4,128,128]{1,2,0:T(8,128)S(1)}, f32[4,128,128]{1,2,0:T(8,128)}, u32[]{:S(2)}) copy-start(f32[4,128,128]{1,2,0:T(8,128)} %custom-call.9) | copy-start | bytes 786436
  481.7 123.5 %all-gather.9.cloned.1.call-start = ((), (), s32[]{:S(2)}) async-start(), calls=%async_computation.4 | async-start | bytes 28311552 | tf_op jit(solution)/shard_map/all_gather | solution.py:76
  483.7 2.0 copy-start.4
Sparse Core Ops, SparseCore 0:
  11.0 25.1 all-gather.10
  37.9 33.0 all-gather.14
  72.6 13.8 all-gather.12
  156.1 88.7 all-reduce.4
  260.4 88.7 all-reduce.6
  364.8 88.6 all-reduce.8
  481.8 88.4 all-reduce.10
Sparse Core Ops, SparseCore 1:
  483.9 121.3 all-gather.8
where the time goes:
time: 746 us; the launch traced here: 737 us
  waiting for transfers between devices  293 us (39%)
  matrix products  188 us (25%)
  other arithmetic  167 us (22%)
  local copies, waits for them, and re-layouts  67.9 us (9%)
  between operations  16.4 us (2%)
    psum x4, waiting for transfers between devices, from_root(): return lax.psum(kept, axis)  198 us
    another operation x6, other arithmetic, local(): lax.linalg.triangular_solve(guarded, right_side, left_side=False, lower=T...  160 us
    dot_general x1, matrix products, local(): jnp.einsum('ms,lts->mlt', solved, masked, precision=lax.Precision.HIGHEST)  124 us
    all_gather x3, waiting for transfers between devices, stacked_from(): pieces = lax.all_gather(pieces, axes[k])  68.6 us
    another operation x85, local copies, waits for them, and re-layouts, local(): lax.linalg.triangular_solve(guarded, right_side, left_side=False, lower=T...  43.8 us
    another operation x28, matrix products, local(): lax.linalg.triangular_solve(guarded, right_side, left_side=False, lower=T...  33.8 us
    dot_general x3, matrix products, local(): jnp.dot(earlier, head_tiles[local_block, :, :step * block_width].T, preci...  30.2 us
    all_gather x1, waiting for transfers between devices, local(): piece = lax.all_gather(factor, ROW, axis=2, tiled=True)  25.7 us
  transfers between devices with their start and end apart: 8, of which 8 were waited for; matrix products, arithmetic and copies ran while one was open for 23% of the time, Pallas kernels for 0%

commit v1 on v0

v1 whole, which is shorter than its diff:
```python
import functools

import jax
import jax.numpy as jnp
from jax import lax
from jax.experimental import pallas as pl
from jax.experimental.pallas import tpu as pltpu
from jax.sharding import Mesh
from jax.sharding import PartitionSpec as P


ROW = ("x", "core")
COL = ("y", "z")
SWAP = [(0, 1), (1, 0)]
HIGHEST = lax.Precision.HIGHEST


def full_dot(a, b):
    return jnp.dot(a, b, precision=HIGHEST, preferred_element_type=jnp.float32)


def dot_nt(a, b):
    return lax.dot_general(
        a, b, (((1,), (1,)), ((), ())), precision=HIGHEST, preferred_element_type=jnp.float32
    )


def inverse_into(tile_ref, out_ref):
    size, wide, small = 512, 128, 16
    parts = size // wide
    diag = jnp.concatenate(
        [tile_ref[wide * p : wide * (p + 1), wide * p : wide * (p + 1)] for p in range(parts)], axis=0
    )
    row = lax.broadcasted_iota(jnp.int32, (size, wide), 0)
    lane = lax.broadcasted_iota(jnp.int32, (size, wide), 1)
    local_row = row % wide
    lower = jnp.where(lane <= local_row, diag, 0.0)
    own = jnp.sum(jnp.where(lane == local_row, lower, 0.0), axis=1, keepdims=True)
    unit = lower / own
    inverse = jnp.where(lane == local_row, 1.0, 0.0)
    block_start = (local_row // small) * small
    inverse = inverse.reshape(size // small, small, wide)
    for i in range(small - 1):
        picked = jnp.where((lane == block_start + i) & (local_row > lane), unit, 0.0)
        weight = jnp.sum(picked, axis=1, keepdims=True).reshape(size // small, small, 1)
        inverse = inverse - weight * inverse[:, i : i + 1, :]
    inverse = inverse.reshape(size, wide)
    r1 = lax.broadcasted_iota(jnp.int32, (wide, wide), 0)
    c1 = lax.broadcasted_iota(jnp.int32, (wide, wide), 1)
    invs = [inverse[wide * p : wide * (p + 1)] for p in range(parts)]
    step = small
    while step < wide:
        keep = (r1 // (2 * step) == c1 // (2 * step)) & (r1 // step > c1 // step)
        offs = [jnp.where(keep, unit[wide * p : wide * (p + 1)], 0.0) for p in range(parts)]
        mids = [full_dot(offs[p], invs[p]) for p in range(parts)]
        invs = [invs[p] - full_dot(invs[p], mids[p]) for p in range(parts)]
        step *= 2
    out_ref[...] = jnp.zeros((size, size), jnp.float32)
    for p in range(parts):
        scale = jnp.broadcast_to(1.0 / own[wide * p : wide * (p + 1)], (wide, wide))
        as_row = jnp.sum(jnp.where(r1 == c1, scale, 0.0), axis=0, keepdims=True)
        out_ref[wide * p : wide * (p + 1), wide * p : wide * (p + 1)] = invs[p] * as_row
    step = wide
    while step < size:
        for s in range(0, size, 2 * step):
            top = out_ref[s : s + step, s : s + step]
            bottom = out_ref[s + step : s + 2 * step, s + step : s + 2 * step]
            between = tile_ref[s + step : s + 2 * step, s : s + step]
            out_ref[s + step : s + 2 * step, s : s + step] = -full_dot(bottom, full_dot(between, top))
        step *= 2


def prepare_body(place_ref, rows_ref, *refs):
    near, far = refs[:4], refs[4:8]
    panel_ref, inverse_ref, first_ref = refs[8:]
    core, y, z = place_ref[0], place_ref[1], place_ref[2]
    for c in range(2):

        @pl.when(core == c)
        def _():
            for d in range(4):
                at = pl.multiple_of(lax.rem(y + (4 - d), 4) * 128, 128)
                for x in range(4):
                    panel_ref[x, pl.ds(at, 128), 256 * c : 256 * (c + 1)] = near[d][x]
                    panel_ref[x, pl.ds(at, 128), 256 * (1 - c) : 256 * (2 - c)] = far[d][x]

    inverse_into(panel_ref.at[z], inverse_ref)
    first_ref[...] = dot_nt(rows_ref[...], inverse_ref[...])


def in_vmem():
    return pl.BlockSpec(memory_space=pltpu.VMEM)


def in_smem():
    return pl.BlockSpec(memory_space=pltpu.SMEM)


def prepare(place, rows, near, far):
    return pl.pallas_call(
        prepare_body,
        in_specs=[in_smem()] + [in_vmem()] * 9,
        out_specs=[in_vmem()] * 3,
        out_shape=[
            jax.ShapeDtypeStruct((4, 512, 512), jnp.float32),
            jax.ShapeDtypeStruct((512, 512), jnp.float32),
            jax.ShapeDtypeStruct((192, 512), jnp.float32),
        ],
        name="prepare",
    )(place, rows, *near, *far)


def step_body(k, place_ref, rows_ref, panel_ref, inverse_ref, own_ref, p1_ref, p2_ref, p3_ref, *outs):
    z = place_ref[2]
    mine_ref = outs[0]
    for d, ref in enumerate((own_ref, p1_ref, p2_ref, p3_ref)):

        @pl.when(z == (k + d) % 4)
        def _():
            mine_ref[...] = ref[...]

    if k < 3:
        rest = rows_ref[...] - dot_nt(mine_ref[...], panel_ref[0])
        outs[1][...] = rest
        outs[2][...] = dot_nt(rest, inverse_ref[...])


def step(k, place, rows, panel, inverse, own, arrived):
    piece = jax.ShapeDtypeStruct((192, 512), jnp.float32)
    count = 3 if k < 3 else 1
    whole = pl.BlockSpec((192, 512), lambda i: (0, 0))
    return pl.pallas_call(
        functools.partial(step_body, k),
        grid=(1,),
        in_specs=[in_smem(), whole, pl.BlockSpec((1, 512, 512), lambda i: (k, 0, 0)), pl.BlockSpec((512, 512), lambda i: (0, 0))]
        + [whole] * 4,
        out_specs=[whole] * count,
        out_shape=[piece] * count,
        name="step",
    )(place, rows, panel, inverse, own, *arrived)


def pack_body(place_ref, own_ref, m1_ref, m2_ref, m3_ref, *rest):
    solved_ref, high_ref, low_ref = rest[-3:]
    core, y = place_ref[0], place_ref[1]
    for d, ref in enumerate((own_ref, m1_ref, m2_ref, m3_ref)):
        at = pl.multiple_of(lax.rem(y + (4 - d), 4) * 192, 192)
        value = ref[...]
        solved_ref[pl.ds(at, 192), :] = value
        left, right = value[:, :256], value[:, 256:]
        value = jnp.concatenate([jnp.where(core == 0, left, right), jnp.where(core == 0, right, left)], axis=1)
        high = value.astype(jnp.bfloat16)
        high_ref[pl.ds(at, 192), :] = high
        low_ref[pl.ds(at, 192), :] = (value - high.astype(jnp.float32)).astype(jnp.bfloat16)


def pack(k, place, pieces, into):
    piece = pl.BlockSpec((192, 512), lambda i: (0, 0))
    column = pl.BlockSpec((768, 512), lambda i: (0, k))
    operands = [place, *pieces]
    specs = [in_smem()] + [piece] * 4
    aliases = {}
    if into is not None:
        operands += into
        specs += [pl.BlockSpec(memory_space=pl.ANY)] * 3
        aliases = {5: 0, 6: 1, 7: 2}
    return pl.pallas_call(
        pack_body,
        grid=(1,),
        in_specs=specs,
        out_specs=[column] * 3,
        out_shape=[jax.ShapeDtypeStruct((768, 2048), t) for t in (jnp.float32, jnp.bfloat16, jnp.bfloat16)],
        input_output_aliases=aliases,
        name="pack",
    )(*operands)


def update_body(first, block_ref, a_ref, xh_ref, xl_ref, own_ref, other_ref, *rest):
    out_ref, high_ref, low_ref = rest[-3:]
    block_id = block_ref[3] + (first + pl.program_id(0)) * 16
    for half, ref in ((0, own_ref), (1, other_ref)):
        for x in range(4):
            at = x * 512 + half * 256
            part = jnp.where(x < block_id, ref[x, 0], 0.0)
            high = part.astype(jnp.bfloat16)
            high_ref[:, at : at + 256] = high
            low_ref[:, at : at + 256] = (part - high.astype(jnp.float32)).astype(jnp.bfloat16)
    dims = (((1,), (1,)), ((), ()))
    high, low = high_ref[...], low_ref[...]
    total = lax.dot_general(xh_ref[...], high, dims, preferred_element_type=jnp.float32)
    total += lax.dot_general(xh_ref[...], low, dims, preferred_element_type=jnp.float32)
    total += lax.dot_general(xl_ref[...], high, dims, preferred_element_type=jnp.float32)
    out_ref[0] = a_ref[0] - total


def update(first, count, block, a, xh, xl, own, other, into=None):
    rows, width = a.shape[1], a.shape[2]
    tb = 256
    big = pl.BlockSpec((1, rows, tb), lambda l, t: (first + l, 0, t))
    tiles = pl.BlockSpec((4, 1, tb, 256), lambda l, t: (0, l, t, 0))
    whole = pl.BlockSpec(xh.shape, lambda l, t: (0, 0))
    operands = [block, a, xh, xl, own, other]
    specs = [pl.BlockSpec(memory_space=pltpu.SMEM), big, whole, whole, tiles, tiles]
    aliases = {}
    if into is not None:
        operands.append(into)
        specs.append(pl.BlockSpec(memory_space=pl.ANY))
        aliases = {6: 0}
    return pl.pallas_call(
        functools.partial(update_body, first),
        grid=(count, width // tb),
        in_specs=specs,
        out_specs=big,
        out_shape=jax.ShapeDtypeStruct(a.shape, jnp.float32),
        scratch_shapes=[pltpu.VMEM((tb, 2048), jnp.bfloat16), pltpu.VMEM((tb, 2048), jnp.bfloat16)],
        input_output_aliases=aliases,
        compiler_params=pltpu.CompilerParams(vmem_limit_bytes=48 * 1024 * 1024),
        name="update",
    )(*operands)


def ring(shift):
    return [(i, (i + shift) % 4) for i in range(4)]


def over_z(value, k):
    return [lax.ppermute(value, "z", [(k, (k + d) % 4)]) for d in (1, 2, 3)]


def over_y(value):
    return [value] + [lax.ppermute(value, "y", ring(d)) for d in (1, 2, 3)]


def placed(matrix, factor):
    core, y, z = lax.axis_index("core"), lax.axis_index("y"), lax.axis_index("z")
    place = jnp.stack([core, y, z, y * 4 + z]).astype(jnp.int32)
    a = matrix.transpose(1, 0, 2)

    def sent(j):
        top = a[0, 192 * j : 192 * (j + 1)]
        return jnp.concatenate([top[:, :256], top[:, 256:], factor[0, 128 * j : 128 * (j + 1)]], axis=0)

    start = sent(0)
    for j in range(1, 4):
        start = jnp.where(y == j, lax.ppermute(sent(j), "y", [(0, j)]), start)
    rows = jnp.concatenate([start[:192], start[192:384]], axis=1)
    tile = lax.all_gather(start[384:], "x")
    near = over_y(tile)
    far = [lax.ppermute(t, "core", SWAP) for t in near]
    panel, inverse, candidate = prepare(place, rows, near, far)

    bulk = []
    for first in (0, 3):
        piece = lax.all_gather(factor[first : first + 3], "x")
        bulk.append((piece, lax.ppermute(piece, "core", SWAP)))

    packed = None
    for k in range(4):
        moved = over_z(candidate, k)
        done = step(k, place, rows, panel, inverse, candidate, moved)
        if k < 3:
            mine, rows, candidate = done
        else:
            mine = done[0]
        pieces = over_y(mine)
        packed = pack(k, place, pieces, packed)
    solved, high, low = packed

    out = update(0, 3, place, a, high, low, *bulk[0])
    out = update(3, 3, place, a, high, low, *bulk[1], out)
    return out.transpose(1, 0, 2), solved


def solution(mesh):
    finer = Mesh(mesh.devices.reshape(4, 2, 4, 4), (*ROW, *COL))
    return jax.shard_map(
        placed,
        mesh=finer,
        in_specs=(P(ROW, None, COL), P(None, COL, ROW)),
        out_specs=(P(ROW, None, COL), P(ROW, None)),
        check_vma=False,
    )
```

time: 746 us -> 410 us (0.55)
  matrix products: 188 us -> 0 us
  other arithmetic: 167 us -> 1.66 us
  Pallas kernels: 0 us -> 79.9 us
  waiting for transfers between devices: 293 us -> 226 us
  starting transfers between devices: 0.54 us -> 62.2 us
  local copies, waits for them, and re-layouts: 67.9 us -> 10.3 us
    psum x4 -> x0, waiting for transfers between devices: 198 us -> none  [from_root(): return lax.psum(kept, axis)]
    another operation x6 -> x1, other arithmetic: 160 us -> 0.61 us  [placed(): place = jnp.stack([core, y, z, y * 4 + z]).astype(jnp.int32)]
    dot_general x4 -> x0, matrix products: 154 us -> none  [the longest x1 124 us: local(): jnp.einsum('ms,lts->mlt', solved, masked, precision=lax.Precision.HIGHEST)]
    ppermute x0 -> x36, waiting for transfers between devices: none -> 92.2 us  [the longest x12 38.8 us: over_z(): return [lax.ppermute(value, 'z', [(k, (k + d) % 4)]) for d in (1, 2, 3)]]
    pallas_call x0 -> x11, Pallas kernels: none -> 79.9 us  [the longest x2 39.7 us: update(): pl.pallas_call(functools.partial(update_body, first), grid=(count, width...]
    ppermute x0 -> x36, starting transfers between devices: none -> 62.1 us  [the longest x15 23.5 us: over_y(): return [value] + [lax.ppermute(value, 'y', ring(d)) for d in (1, 2, 3)]]
    another operation x85 -> x0, local copies, waits for them, and re-layouts: 43.8 us -> none  [local(): lax.linalg.triangular_solve(guarded, right_side, left_side=False, lower=T...]
    all_gather x4 -> x2, waiting for transfers between devices: 94.3 us -> 133 us  [placed(): piece = lax.all_gather(factor[first:first + 3], 'x')]
  transfers between devices with their start and end apart: 8 -> 38, of which waited for: 8 -> 18; matrix products, arithmetic and copies ran while one was open for 23% -> 1% of each run, Pallas kernels for 0% -> 15%
where the time goes in v1:
time: 410 us; the launch traced here: 405 us
  waiting for transfers between devices  226 us (55%)
  Pallas kernels  79.9 us (19%)
  starting transfers between devices  62.2 us (15%)
  between operations  14.4 us (4%)
  local copies, waits for them, and re-layouts  10.3 us (3%)
  blocking collectives  10.2 us (2%)
    all_gather x2, waiting for transfers between devices, placed(): piece = lax.all_gather(factor[first:first + 3], 'x')  133 us
    pallas_call x2, Pallas kernels, update(): pl.pallas_call(functools.partial(update_body, first), grid=(count, width...  39.7 us
    ppermute x12, waiting for transfers between devices, over_z(): return [lax.ppermute(value, 'z', [(k, (k + d) % 4)]) for d in (1, 2, 3)]  38.8 us
    ppermute x15, waiting for transfers between devices, over_y(): return [value] + [lax.ppermute(value, 'y', ring(d)) for d in (1, 2, 3)]  34.2 us
    ppermute x15, starting transfers between devices, over_y(): return [value] + [lax.ppermute(value, 'y', ring(d)) for d in (1, 2, 3)]  23.5 us
    pallas_call x4, Pallas kernels, step(): pl.pallas_call(functools.partial(step_body, k), grid=(1,), in_specs=[in_s...  18.4 us
    ppermute x3, waiting for transfers between devices, placed(): start = jnp.where(y == j, lax.ppermute(sent(j), 'y', [(0, j)]), start)  18 us
    ppermute x12, starting transfers between devices, over_z(): return [lax.ppermute(value, 'z', [(k, (k + d) % 4)]) for d in (1, 2, 3)]  16.2 us
  transfers between devices with their start and end apart: 38, of which 18 were waited for; matrix products, arithmetic and copies ran while one was open for 1% of the time, Pallas kernels for 15%

profile of v1, /device:TPU:1, one launch (start us, length us, event | category | flops | bytes accessed | tf_op | source)
XLA Modules:
  0.0 404.5 jit_solution(2498663805265441959)
XLA Ops:
  7.2 3.9 fusion.2
  13.1 1.5 slice_bitcast_fusion
  14.6 65.3 %all-gather.8.cloned.1.call-done = f32[12,512,256]{2,1,0:T(8,128)} async-done(((f32[3,512,256]{2,1,0:T(8,128)}), f32[12,512,256]{2,1,0:T(8,128)}) %all-gather.8.cloned.1.call-update) | async-done | bytes 6291472 | tf_op jit(solution)/shard_map/all_gather | solution.py:254
  80.8 67.7 %all-gather.6.cloned.1.call-done = f32[12,512,256]{2,1,0:T(8,128)} async-done(((f32[3,512,256]{2,1,0:T(8,128)}), f32[12,512,256]{2,1,0:T(8,128)}) %all-gather.6.cloned.1.call-update) | async-done | bytes 6291472 | tf_op jit(solution)/shard_map/all_gather | solution.py:254
  149.4 3.1 collective-permute-start.2
  152.6 2.2 collective-permute-start.1
  154.9 2.1 collective-permute-start
  157.0 6.8 %collective-permute-done.2 = f32[512,256]{1,0:T(8,128)S(1)} collective-permute-done((f32[512,256]{1,0:T(8,128)S(1)}, f32[512,256]{1,0:T(8,128)S(1)}, u32[]{:S(2)}, u32[]{:S(2)}) %collective-permute-start.2) | collective-permute-done | bytes 524320 | tf_op jit(solution)/shard_map/ppermute | solution.py:245
  163.7 11.2 %collective-permute-done.1 = f32[512,256]{1,0:T(8,128)S(1)} collective-permute-done((f32[512,256]{1,0:T(8,128)S(1)}, f32[512,256]{1,0:T(8,128)S(1)}, u32[]{:S(2)}, u32[]{:S(2)}) %collective-permute-start.1) | collective-permute-done | bytes 524320 | tf_op jit(solution)/shard_map/ppermute | solution.py:245
  175.1 10.2 %all-gather = f32[512,256]{1,0:T(8,128)S(1)} all-gather(f32[128,256]{1,0:T(8,128)S(1)} %slice.98), channel_id=2, replica_groups=mesh['x'=4,'core'=2,'y'=4,'z'=4] {'x'}, dimensions={0}, use_global_device_ids=true | all-gather | bytes 655360 | tf_op jit(solution)/shard_map/all_gather | solution.py:247
  185.3 3.7 collective-permute-start.4
  189.1 2.0 collective-permute-start.5
  191.1 4.8 %collective-permute-done.3.refs_1_ = f32[4,128,256]{2,1,0:T(8,128)S(1)} collective-permute-done((f32[4,128,256]{2,1,0:T(8,128)S(1)}, f32[4,128,256]{2,1,0:T(8,128)S(1)}, u32[]{:S(2)}, u32[]{:S(2)}) %collective-permute-start.3) | collective-permute-done | bytes 524320 | tf_op jit(solution)/shard_map/ppermute | solution.py:231
  195.9 8.1 %collective-permute-start.6 = (f32[4,128,256]{2,1,0:T(8,128)S(1)}, f32[4,128,256]{2,1,0:T(8,128)S(1)}, u32[]{:S(2)}, u32[]{:S(2)}) collective-permute-start(f32[4,128,256]{2,1,0:T(8,128)S(1)} %bitcast.36), channel_id=1, source_target_pairs={{0,16},{16,0},{1,17},{17,1},{2,18},{18,2},{3,19},{19,3},{4,20},{20... | collective-permute-start | bytes 1572872 | tf_op jit(solution)/shard_map/ppermute | solution.py:249
  204.1 4.4 %collective-permute-done.4.refs_2_ = f32[4,128,256]{2,1,0:T(8,128)S(1)} collective-permute-done((f32[4,128,256]{2,1,0:T(8,128)S(1)}, f32[4,128,256]{2,1,0:T(8,128)S(1)}, u32[]{:S(2)}, u32[]{:S(2)}) %collective-permute-start.4) | collective-permute-done | bytes 524320 | tf_op jit(solution)/shard_map/ppermute | solution.py:231
  208.5 4.7 %collective-permute-start.7 = (f32[4,128,256]{2,1,0:T(8,128)S(1)}, f32[4,128,256]{2,1,0:T(8,128)}, u32[]{:S(2)}, u32[]{:S(2)}) collective-permute-start(f32[4,128,256]{2,1,0:T(8,128)S(1)} %collective-permute-done.3.refs_1_), channel_id=1, source_target_pairs={{0,16},{16,0},{1,17},{17,1},{2,18},{18,2},{3,19},{19,3},{4,20},{20... | collective-permute-start | bytes 1572872 | tf_op jit(solution)/shard_map/ppermute | solution.py:249
  216.3 8.3 %prepare.1 = (f32[4,512,512]{2,1,0:T(8,128)}, f32[512,512]{1,0:T(8,128)}, f32[192,512]{1,0:T(8,128)}) custom-call(s32[4]{0:T(128)} %pad_add_fusion.place_ref.block_ref, f32[192,512]{1,0:T(8,128)} %pad_maximum_fusion.3.rows_ref, f32[4,128,256]{2,1,0:T(8,128)} %bitcast.37, f32[4,128,256]{2,1,0:T(8,128)} %copy-done.3, f32[4,128,256]{2,1,0:T(8,128)} %copy-done.4, ...), custom_call_target="tpu_custom_call" | custom-call | tf_op jit(solution)/shard_map/prepare/pallas_call | solution.py:100
  224.6 3.2 collective-permute-start.10
  227.8 2.3 collective-permute-start.11
  230.1 1.3 collective-permute-start.12
  231.4 4.8 %collective-permute-done.10.p1_ref = f32[192,512]{1,0:T(8,128)S(1)} collective-permute-done((f32[192,512]{1,0:T(8,128)}, f32[192,512]{1,0:T(8,128)S(1)}, u32[]{:S(2)}, u32[]{:S(2)}) %collective-permute-start.10) | collective-permute-done | bytes 393248 | tf_op jit(solution)/shard_map/ppermute | solution.py:227
  236.2 8.4 %collective-permute-done.11.p2_ref = f32[192,512]{1,0:T(8,128)S(1)} collective-permute-done((f32[192,512]{1,0:T(8,128)}, f32[192,512]{1,0:T(8,128)S(1)}, u32[]{:S(2)}, u32[]{:S(2)}) %collective-permute-start.11) | collective-permute-done | bytes 393248 | tf_op jit(solution)/shard_map/ppermute | solution.py:227
  245.5 5.2 %step.4 = (f32[192,512]{1,0:T(8,128)}, f32[192,512]{1,0:T(8,128)}, f32[192,512]{1,0:T(8,128)}) custom-call(s32[4]{0:T(128)} %pad_add_fusion.place_ref.block_ref, f32[192,512]{1,0:T(8,128)} %pad_maximum_fusion.3.rows_ref, f32[4,512,512]{2,1,0:T(8,128)} %get-tuple-element.26.panel_ref, f32[512,512]{1,0:T(8,128)} %get-tuple-element.27.inverse_ref, ...), custom_call_target="tpu_custom_call" | custom-call | tf_op jit(solution)/shard_map/step/pallas_call | solution.py:132
  252.0 1.3 collective-permute-start.15
  254.0 2.3 collective-permute-start.32
  256.2 17.5 %collective-permute-done.15.p3_ref = f32[192,512]{1,0:T(8,128)S(1)} collective-permute-done((f32[192,512]{1,0:T(8,128)}, f32[192,512]{1,0:T(8,128)S(1)}, u32[]{:S(2)}, u32[]{:S(2)}) %collective-permute-start.15) | collective-permute-done | bytes 393248 | tf_op jit(solution)/shard_map/ppermute | solution.py:227
  273.7 1.3 collective-permute-start.33
  275.1 5.1 %step.5 = (f32[192,512]{1,0:T(8,128)}, f32[192,512]{1,0:T(8,128)}, f32[192,512]{1,0:T(8,128)}) custom-call(s32[4]{0:T(128)} %pad_add_fusion.place_ref.block_ref, f32[192,512]{1,0:T(8,128)} %get-tuple-element.29.rows_ref, f32[4,512,512]{2,1,0:T(8,128)} %get-tuple-element.26.panel_ref, f32[512,512]{1,0:T(8,128)} %get-tuple-element.27.inverse_ref, ...), custom_call_target="tpu_custom_call" | custom-call | tf_op jit(solution)/shard_map/step/pallas_call | solution.py:132
  280.9 1.3 collective-permute-start.17
  284.5 8.1 %collective-permute-done.17.p2_ref = f32[192,512]{1,0:T(8,128)S(1)} collective-permute-done((f32[192,512]{1,0:T(8,128)}, f32[192,512]{1,0:T(8,128)S(1)}, u32[]{:S(2)}, u32[]{:S(2)}) %collective-permute-start.17) | collective-permute-done | bytes 393248 | tf_op jit(solution)/shard_map/ppermute | solution.py:227
  292.6 2.6 collective-permute-start.29
  296.3 5.2 %step.6 = (f32[192,512]{1,0:T(8,128)}, f32[192,512]{1,0:T(8,128)}, f32[192,512]{1,0:T(8,128)}) custom-call(s32[4]{0:T(128)} %pad_add_fusion.place_ref.block_ref, f32[192,512]{1,0:T(8,128)} %get-tuple-element.31.rows_ref, f32[4,512,512]{2,1,0:T(8,128)} %get-tuple-element.26.panel_ref, f32[512,512]{1,0:T(8,128)} %get-tuple-element.27.inverse_ref, ...), custom_call_target="tpu_custom_call" | custom-call | tf_op jit(solution)/shard_map/step/pallas_call | solution.py:132
  301.5 1.3 collective-permute-start.19
  302.8 1.4 collective-permute-start.20
  304.2 8.3 %collective-permute-done.30.m3_ref = f32[192,512]{1,0:T(8,128)S(1)} collective-permute-done((f32[192,512]{1,0:T(8,128)}, f32[192,512]{1,0:T(8,128)S(1)}, u32[]{:S(2)}, u32[]{:S(2)}) %collective-permute-start.30) | collective-permute-done | bytes 393248 | tf_op jit(solution)/shard_map/ppermute | solution.py:231
  312.6 1.4 collective-permute-start.21
  314.3 4.2 %collective-permute-start.26 = (f32[192,512]{1,0:T(8,128)}, f32[192,512]{1,0:T(8,128)S(1)}, u32[]{:S(2)}, u32[]{:S(2)}) collective-permute-start(f32[192,512]{1,0:T(8,128)} %get-tuple-element.35.own_ref), channel_id=1, source_target_pairs={{0,8},{4,12},{8,0},{12,4},{1,9},{5,13},{9,1},{13,5},{2,10},{6,14},... | collective-permute-start | bytes 1179656 | tf_op jit(solution)/shard_map/ppermute | solution.py:231
  318.5 2.9 step.7.own_ref
  323.0 10.3 %collective-permute-done.26.m2_ref = f32[192,512]{1,0:T(8,128)S(1)} collective-permute-done((f32[192,512]{1,0:T(8,128)}, f32[192,512]{1,0:T(8,128)S(1)}, u32[]{:S(2)}, u32[]{:S(2)}) %collective-permute-start.26) | collective-permute-done | bytes 393248 | tf_op jit(solution)/shard_map/ppermute | solution.py:231
  333.2 3.8 collective-permute-done.27.m3_ref
  337.0 3.8 collective-permute-start.24
  340.8 3.4 pack.4
  344.2 3.4 pack.5
  347.6 3.4 pack.6
  352.7 3.4 pack.7
  356.1 1.9 copy-done
  358.0 19.8 %update.2.rest_0_ = f32[6,768,512]{2,1,0:T(8,128)} custom-call(s32[4]{0:T(128)S(1)} %copy-done.1, f32[6,768,512]{2,1,0:T(8,128)} %bitcast.26, bf16[768,2048]{1,0:T(8,128)(2,1)S(1)} %copy-done, bf16[768,2048]{1,0:T(8,128)(2,1)} %get-tuple-element.48.xl_ref, f32[4,3,512,256]{3,2,1,0:T(8,128)} %bitcast.30, f32[4,3,512,256]{3,2,1,0:T(8,128)} %collective-permute-done.35.other_ref), custom_call_target="tpu_custom_call" | custom-call | tf_op jit(solution)/shard_map/update/pallas_call | solution.py:209
  377.8 19.9 %update.3 = f32[6,768,512]{2,1,0:T(8,128)} custom-call(s32[4]{0:T(128)S(1)} %copy-done.1, f32[6,768,512]{2,1,0:T(8,128)} %bitcast.27, bf16[768,2048]{1,0:T(8,128)(2,1)S(1)} %copy-done, bf16[768,2048]{1,0:T(8,128)(2,1)} %get-tuple-element.48.xl_ref, f32[4,3,512,256]{3,2,1,0:T(8,128)} %bitcast.32, ...), custom_call_target="tpu_custom_call", output_to_operand_aliasing={{}: (6, {})} | custom-call | tf_op jit(solution)/shard_map/update/pallas_call | solution.py:209
  (112 shorter events, 17.7 us)
Async XLA Ops:
  7.2 72.8 %all-gather.8.cloned.1.call-start = ((), (), s32[]{:S(2)}) async-start(), calls=%async_computation.1 | async-start | bytes 7864320 | tf_op jit(solution)/shard_map/all_gather | solution.py:254
  11.2 137.3 %all-gather.6.cloned.1.call-start = ((), (), s32[]{:S(2)}) async-start(), calls=%async_computation | async-start | bytes 7864320 | tf_op jit(solution)/shard_map/all_gather | solution.py:254
  80.0 276.1 %collective-permute-start.35 = (f32[4,3,512,256]{3,2,1,0:T(8,128)}, f32[4,3,512,256]{3,2,1,0:T(8,128)}, u32[]{:S(2)}, u32[]{:S(2)}) collective-permute-start(f32[4,3,512,256]{3,2,1,0:T(8,128)} %bitcast.29), channel_id=1, source_target_pairs={{0,16},{16,0},{1,17},{17,1},{2,18},{18,2},{3,19},{19,3},{4,20},{20... | collective-permute-start | bytes 18874376 | tf_op jit(solution)/shard_map/ppermute | solution.py:255
  148.5 229.3 %collective-permute-start.34 = (f32[4,3,512,256]{3,2,1,0:T(8,128)}, f32[4,3,512,256]{3,2,1,0:T(8,128)}, u32[]{:S(2)}, u32[]{:S(2)}) collective-permute-start(f32[4,3,512,256]{3,2,1,0:T(8,128)} %bitcast.31), channel_id=1, source_target_pairs={{0,16},{16,0},{1,17},{17,1},{2,18},{18,2},{3,19},{19,3},{4,20},{20... | collective-permute-start | bytes 18874376 | tf_op jit(solution)/shard_map/ppermute | solution.py:255
  149.4 14.4 %collective-permute-start.2 = (f32[512,256]{1,0:T(8,128)S(1)}, f32[512,256]{1,0:T(8,128)S(1)}, u32[]{:S(2)}, u32[]{:S(2)}) collective-permute-start(f32[512,256]{1,0:T(8,128)S(1)} %pad_maximum_fusion.2), channel_id=1, source_target_pairs={{0,4},{1,5},{2,6},{3,7},{16,20},{17,21},{18,22},{19,23},{32,36},{3... | collective-permute-start | bytes 1572872 | tf_op jit(solution)/shard_map/ppermute | solution.py:245
  152.6 22.4 %collective-permute-start.1 = (f32[512,256]{1,0:T(8,128)S(1)}, f32[512,256]{1,0:T(8,128)S(1)}, u32[]{:S(2)}, u32[]{:S(2)}) collective-permute-start(f32[512,256]{1,0:T(8,128)S(1)} %pad_maximum_fusion.1), channel_id=1, source_target_pairs={{0,8},{1,9},{2,10},{3,11},{16,24},{17,25},{18,26},{19,27},{32,40},... | collective-permute-start | bytes 1572872 | tf_op jit(solution)/shard_map/ppermute | solution.py:245
  154.9 20.1 %collective-permute-start = (f32[512,256]{1,0:T(8,128)S(1)}, f32[512,256]{1,0:T(8,128)}, u32[]{:S(2)}, u32[]{:S(2)}) collective-permute-start(f32[512,256]{1,0:T(8,128)S(1)} %pad_maximum_fusion), channel_id=1, source_target_pairs={{0,12},{1,13},{2,14},{3,15},{16,28},{17,29},{18,30},{19,31},{32,44... | collective-permute-start | bytes 1572872 | tf_op jit(solution)/shard_map/ppermute | solution.py:245
  185.3 31.0 %copy-start.2 = (f32[512,256]{1,0:T(8,128)}, f32[512,256]{1,0:T(8,128)S(1)}, u32[]{:S(2)}) copy-start(f32[512,256]{1,0:T(8,128)S(1)} %all-gather) | copy-start | bytes 1572868
  185.3 10.6 %collective-permute-start.3 = (f32[4,128,256]{2,1,0:T(8,128)S(1)}, f32[4,128,256]{2,1,0:T(8,128)S(1)}, u32[]{:S(2)}, u32[]{:S(2)}) collective-permute-start(f32[4,128,256]{2,1,0:T(8,128)S(1)} %bitcast.33), channel_id=1, source_target_pairs={{0,4},{4,8},{8,12},{12,0},{1,5},{5,9},{9,13},{13,1},{2,6},{6,10},{... | collective-permute-start | bytes 1572872 | tf_op jit(solution)/shard_map/ppermute | solution.py:231
  185.3 23.2 %collective-permute-start.4 = (f32[4,128,256]{2,1,0:T(8,128)S(1)}, f32[4,128,256]{2,1,0:T(8,128)S(1)}, u32[]{:S(2)}, u32[]{:S(2)}) collective-permute-start(f32[4,128,256]{2,1,0:T(8,128)S(1)} %bitcast.34), channel_id=1, source_target_pairs={{0,8},{4,12},{8,0},{12,4},{1,9},{5,13},{9,1},{13,5},{2,10},{6,14},... | collective-permute-start | bytes 1572872 | tf_op jit(solution)/shard_map/ppermute | solution.py:231
  189.1 24.1 %collective-permute-start.5 = (f32[4,128,256]{2,1,0:T(8,128)S(1)}, f32[4,128,256]{2,1,0:T(8,128)S(1)}, u32[]{:S(2)}, u32[]{:S(2)}) collective-permute-start(f32[4,128,256]{2,1,0:T(8,128)S(1)} %bitcast.35), channel_id=1, source_target_pairs={{0,12},{4,0},{8,4},{12,8},{1,13},{5,1},{9,5},{13,9},{2,14},{6,2},{... | collective-permute-start | bytes 1572872 | tf_op jit(solution)/shard_map/ppermute | solution.py:231
  195.9 20.4 %copy-start.3 = (f32[4,128,256]{2,1,0:T(8,128)}, f32[4,128,256]{2,1,0:T(8,128)S(1)}, u32[]{:S(2)}) copy-start(f32[4,128,256]{2,1,0:T(8,128)S(1)} %collective-permute-done.3.refs_1_) | copy-start | bytes 1572868
  195.9 17.3 %collective-permute-start.6 = (f32[4,128,256]{2,1,0:T(8,128)S(1)}, f32[4,128,256]{2,1,0:T(8,128)S(1)}, u32[]{:S(2)}, u32[]{:S(2)}) collective-permute-start(f32[4,128,256]{2,1,0:T(8,128)S(1)} %bitcast.36), channel_id=1, source_target_pairs={{0,16},{16,0},{1,17},{17,1},{2,18},{18,2},{3,19},{19,3},{4,20},{20... | collective-permute-start | bytes 1572872 | tf_op jit(solution)/shard_map/ppermute | solution.py:249
  208.5 6.6 %collective-permute-start.7 = (f32[4,128,256]{2,1,0:T(8,128)S(1)}, f32[4,128,256]{2,1,0:T(8,128)}, u32[]{:S(2)}, u32[]{:S(2)}) collective-permute-start(f32[4,128,256]{2,1,0:T(8,128)S(1)} %collective-permute-done.3.refs_1_), channel_id=1, source_target_pairs={{0,16},{16,0},{1,17},{17,1},{2,18},{18,2},{3,19},{19,3},{4,20},{20... | collective-permute-start | bytes 1572872 | tf_op jit(solution)/shard_map/ppermute | solution.py:249
  213.1 2.4 collective-permute-start.8
  213.2 3.1 collective-permute-start.9
  224.6 11.6 %collective-permute-start.10 = (f32[192,512]{1,0:T(8,128)}, f32[192,512]{1,0:T(8,128)S(1)}, u32[]{:S(2)}, u32[]{:S(2)}) collective-permute-start(f32[192,512]{1,0:T(8,128)} %get-tuple-element.28.own_ref), channel_id=1, source_target_pairs={{0,1},{4,5},{8,9},{12,13},{16,17},{20,21},{24,25},{28,29},{32,33},... | collective-permute-start | bytes 1179656 | tf_op jit(solution)/shard_map/ppermute | solution.py:227
  227.8 16.8 %collective-permute-start.11 = (f32[192,512]{1,0:T(8,128)}, f32[192,512]{1,0:T(8,128)S(1)}, u32[]{:S(2)}, u32[]{:S(2)}) collective-permute-start(f32[192,512]{1,0:T(8,128)} %get-tuple-element.28.own_ref), channel_id=1, source_target_pairs={{0,2},{4,6},{8,10},{12,14},{16,18},{20,22},{24,26},{28,30},{32,34}... | collective-permute-start | bytes 1179656 | tf_op jit(solution)/shard_map/ppermute | solution.py:227
  230.1 14.5 %collective-permute-start.12 = (f32[192,512]{1,0:T(8,128)}, f32[192,512]{1,0:T(8,128)S(1)}, u32[]{:S(2)}, u32[]{:S(2)}) collective-permute-start(f32[192,512]{1,0:T(8,128)} %get-tuple-element.28.own_ref), channel_id=1, source_target_pairs={{0,3},{4,7},{8,11},{12,15},{16,19},{20,23},{24,27},{28,31},{32,35}... | collective-permute-start | bytes 1179656 | tf_op jit(solution)/shard_map/ppermute | solution.py:227
  250.6 2.7 collective-permute-start.13
  251.3 2.6 collective-permute-start.14
  252.0 21.7 %collective-permute-start.15 = (f32[192,512]{1,0:T(8,128)}, f32[192,512]{1,0:T(8,128)S(1)}, u32[]{:S(2)}, u32[]{:S(2)}) collective-permute-start(f32[192,512]{1,0:T(8,128)} %get-tuple-element.30.own_ref), channel_id=1, source_target_pairs={{1,0},{5,4},{9,8},{13,12},{17,16},{21,20},{25,24},{29,28},{33,32},... | collective-permute-start | bytes 1179656 | tf_op jit(solution)/shard_map/ppermute | solution.py:227
  253.3 21.7 %copy-start.17 = (f32[192,512]{1,0:T(8,128)}, f32[192,512]{1,0:T(8,128)S(1)}, u32[]{:S(2)}) copy-start(f32[192,512]{1,0:T(8,128)S(1)} %collective-permute-done.13.p1_ref) | copy-start | bytes 1179652
  253.3 26.9 %collective-permute-start.31 = (f32[192,512]{1,0:T(8,128)}, f32[192,512]{1,0:T(8,128)S(1)}, u32[]{:S(2)}, u32[]{:S(2)}) collective-permute-start(f32[192,512]{1,0:T(8,128)} %get-tuple-element.37.own_ref), channel_id=1, source_target_pairs={{0,4},{4,8},{8,12},{12,0},{1,5},{5,9},{9,13},{13,1},{2,6},{6,10},{... | collective-permute-start | bytes 1179656 | tf_op jit(solution)/shard_map/ppermute | solution.py:231
  254.0 21.1 %copy-start.19 = (f32[192,512]{1,0:T(8,128)}, f32[192,512]{1,0:T(8,128)S(1)}, u32[]{:S(2)}) copy-start(f32[192,512]{1,0:T(8,128)S(1)} %collective-permute-done.14.p2_ref) | copy-start | bytes 1179652
  254.0 26.9 %collective-permute-start.32 = (f32[192,512]{1,0:T(8,128)}, f32[192,512]{1,0:T(8,128)S(1)}, u32[]{:S(2)}, u32[]{:S(2)}) collective-permute-start(f32[192,512]{1,0:T(8,128)} %get-tuple-element.37.own_ref), channel_id=1, source_target_pairs={{0,8},{4,12},{8,0},{12,4},{1,9},{5,13},{9,1},{13,5},{2,10},{6,14},... | collective-permute-start | bytes 1179656 | tf_op jit(solution)/shard_map/ppermute | solution.py:231
  273.7 8.9 %collective-permute-start.33 = (f32[192,512]{1,0:T(8,128)}, f32[192,512]{1,0:T(8,128)}, u32[]{:S(2)}, u32[]{:S(2)}) collective-permute-start(f32[192,512]{1,0:T(8,128)} %get-tuple-element.37.own_ref), channel_id=1, source_target_pairs={{0,12},{4,0},{8,4},{12,8},{1,13},{5,1},{9,5},{13,9},{2,14},{6,2},{... | collective-permute-start | bytes 1179656 | tf_op jit(solution)/shard_map/ppermute | solution.py:231
  280.2 60.6 %copy-start.25 = (f32[192,512]{1,0:T(8,128)}, f32[192,512]{1,0:T(8,128)S(1)}, u32[]{:S(2)}) copy-start(f32[192,512]{1,0:T(8,128)S(1)} %collective-permute-done.31.m1_ref) | copy-start | bytes 1179652
  280.2 3.1 collective-permute-start.16
  280.9 59.9 %copy-start.26 = (f32[192,512]{1,0:T(8,128)}, f32[192,512]{1,0:T(8,128)S(1)}, u32[]{:S(2)}) copy-start(f32[192,512]{1,0:T(8,128)S(1)} %collective-permute-done.32.m2_ref) | copy-start | bytes 1179652
  280.9 11.6 %collective-permute-start.17 = (f32[192,512]{1,0:T(8,128)}, f32[192,512]{1,0:T(8,128)S(1)}, u32[]{:S(2)}, u32[]{:S(2)}) collective-permute-start(f32[192,512]{1,0:T(8,128)} %get-tuple-element.32.own_ref), channel_id=1, source_target_pairs={{2,0},{6,4},{10,8},{14,12},{18,16},{22,20},{26,24},{30,28},{34,32}... | collective-permute-start | bytes 1179656 | tf_op jit(solution)/shard_map/ppermute | solution.py:227
  282.6 12.5 %collective-permute-start.18 = (f32[192,512]{1,0:T(8,128)}, f32[192,512]{1,0:T(8,128)S(1)}, u32[]{:S(2)}, u32[]{:S(2)}) collective-permute-start(f32[192,512]{1,0:T(8,128)} %get-tuple-element.32.own_ref), channel_id=1, source_target_pairs={{2,1},{6,5},{10,9},{14,13},{18,17},{22,21},{26,25},{30,29},{34,33}... | collective-permute-start | bytes 1179656 | tf_op jit(solution)/shard_map/ppermute | solution.py:227
  283.3 18.1 %collective-permute-start.28 = (f32[192,512]{1,0:T(8,128)}, f32[192,512]{1,0:T(8,128)S(1)}, u32[]{:S(2)}, u32[]{:S(2)}) collective-permute-start(f32[192,512]{1,0:T(8,128)} %get-tuple-element.36.own_ref), channel_id=1, source_target_pairs={{0,4},{4,8},{8,12},{12,0},{1,5},{5,9},{9,13},{13,1},{2,6},{6,10},{... | collective-permute-start | bytes 1179656 | tf_op jit(solution)/shard_map/ppermute | solution.py:231
  292.6 10.2 %collective-permute-start.29 = (f32[192,512]{1,0:T(8,128)}, f32[192,512]{1,0:T(8,128)S(1)}, u32[]{:S(2)}, u32[]{:S(2)}) collective-permute-start(f32[192,512]{1,0:T(8,128)} %get-tuple-element.36.own_ref), channel_id=1, source_target_pairs={{0,8},{4,12},{8,0},{12,4},{1,9},{5,13},{9,1},{13,5},{2,10},{6,14},... | collective-permute-start | bytes 1179656 | tf_op jit(solution)/shard_map/ppermute | solution.py:231
  295.2 17.4 %collective-permute-start.30 = (f32[192,512]{1,0:T(8,128)}, f32[192,512]{1,0:T(8,128)S(1)}, u32[]{:S(2)}, u32[]{:S(2)}) collective-permute-start(f32[192,512]{1,0:T(8,128)} %get-tuple-element.36.own_ref), channel_id=1, source_target_pairs={{0,12},{4,0},{8,4},{12,8},{1,13},{5,1},{9,5},{13,9},{2,14},{6,2},{... | collective-permute-start | bytes 1179656 | tf_op jit(solution)/shard_map/ppermute | solution.py:231
  301.5 19.9 %copy-start.7 = (f32[192,512]{1,0:T(8,128)}, f32[192,512]{1,0:T(8,128)S(1)}, u32[]{:S(2)}) copy-start(f32[192,512]{1,0:T(8,128)S(1)} %collective-permute-done.28.m1_ref) | copy-start | bytes 1179652
  301.5 12.5 %collective-permute-start.19 = (f32[192,512]{1,0:T(8,128)}, f32[192,512]{1,0:T(8,128)S(1)}, u32[]{:S(2)}, u32[]{:S(2)}) collective-permute-start(f32[192,512]{1,0:T(8,128)} %get-tuple-element.34.own_ref), channel_id=1, source_target_pairs={{3,0},{7,4},{11,8},{15,12},{19,16},{23,20},{27,24},{31,28},{35,32}... | collective-permute-start | bytes 1179656 | tf_op jit(solution)/shard_map/ppermute | solution.py:227
  302.8 18.6 %copy-start.8 = (f32[192,512]{1,0:T(8,128)}, f32[192,512]{1,0:T(8,128)S(1)}, u32[]{:S(2)}) copy-start(f32[192,512]{1,0:T(8,128)S(1)} %collective-permute-done.29.m2_ref) | copy-start | bytes 1179652
  302.8 11.5 %collective-permute-start.20 = (f32[192,512]{1,0:T(8,128)}, f32[192,512]{1,0:T(8,128)}, u32[]{:S(2)}, u32[]{:S(2)}) collective-permute-start(f32[192,512]{1,0:T(8,128)} %get-tuple-element.34.own_ref), channel_id=1, source_target_pairs={{3,1},{7,5},{11,9},{15,13},{19,17},{23,21},{27,25},{31,29},{35,33}... | collective-permute-start | bytes 1179656 | tf_op jit(solution)/shard_map/ppermute | solution.py:227
  312.6 5.9 %collective-permute-start.21 = (f32[192,512]{1,0:T(8,128)}, f32[192,512]{1,0:T(8,128)}, u32[]{:S(2)}, u32[]{:S(2)}) collective-permute-start(f32[192,512]{1,0:T(8,128)} %get-tuple-element.34.own_ref), channel_id=1, source_target_pairs={{3,2},{7,6},{11,10},{15,14},{19,18},{23,22},{27,26},{31,30},{35,34... | collective-permute-start | bytes 1179656 | tf_op jit(solution)/shard_map/ppermute | solution.py:227
  314.0 8.7 %collective-permute-start.25 = (f32[192,512]{1,0:T(8,128)}, f32[192,512]{1,0:T(8,128)S(1)}, u32[]{:S(2)}, u32[]{:S(2)}) collective-permute-start(f32[192,512]{1,0:T(8,128)} %get-tuple-element.35.own_ref), channel_id=1, source_target_pairs={{0,4},{4,8},{8,12},{12,0},{1,5},{5,9},{9,13},{13,1},{2,6},{6,10},{... | collective-permute-start | bytes 1179656 | tf_op jit(solution)/shard_map/ppermute | solution.py:231
  314.3 19.0 %collective-permute-start.26 = (f32[192,512]{1,0:T(8,128)}, f32[192,512]{1,0:T(8,128)S(1)}, u32[]{:S(2)}, u32[]{:S(2)}) collective-permute-start(f32[192,512]{1,0:T(8,128)} %get-tuple-element.35.own_ref), channel_id=1, source_target_pairs={{0,8},{4,12},{8,0},{12,4},{1,9},{5,13},{9,1},{13,5},{2,10},{6,14},... | collective-permute-start | bytes 1179656 | tf_op jit(solution)/shard_map/ppermute | solution.py:231
  318.5 18.5 %collective-permute-start.27 = (f32[192,512]{1,0:T(8,128)}, f32[192,512]{1,0:T(8,128)S(1)}, u32[]{:S(2)}, u32[]{:S(2)}) collective-permute-start(f32[192,512]{1,0:T(8,128)} %get-tuple-element.35.own_ref), channel_id=1, source_target_pairs={{0,12},{4,0},{8,4},{12,8},{1,13},{5,1},{9,5},{13,9},{2,14},{6,2},{... | collective-permute-start | bytes 1179656 | tf_op jit(solution)/shard_map/ppermute | solution.py:231
  322.6 24.9 %copy-start.10 = (f32[192,512]{1,0:T(8,128)}, f32[192,512]{1,0:T(8,128)S(1)}, u32[]{:S(2)}) copy-start(f32[192,512]{1,0:T(8,128)S(1)} %collective-permute-done.25.m1_ref) | copy-start | bytes 1179652
  322.6 28.4 %collective-permute-start.22 = (f32[192,512]{1,0:T(8,128)}, f32[192,512]{1,0:T(8,128)S(1)}, u32[]{:S(2)}, u32[]{:S(2)}) collective-permute-start(f32[192,512]{1,0:T(8,128)} %step.7.own_ref), channel_id=1, source_target_pairs={{0,4},{4,8},{8,12},{12,0},{1,5},{5,9},{9,13},{13,1},{2,6},{6,10},{... | collective-permute-start | bytes 1179656 | tf_op jit(solution)/shard_map/ppermute | solution.py:231
  333.2 14.3 %copy-start.11 = (f32[192,512]{1,0:T(8,128)}, f32[192,512]{1,0:T(8,128)S(1)}, u32[]{:S(2)}) copy-start(f32[192,512]{1,0:T(8,128)S(1)} %collective-permute-done.26.m2_ref) | copy-start | bytes 1179652
  333.2 17.8 %collective-permute-start.23 = (f32[192,512]{1,0:T(8,128)}, f32[192,512]{1,0:T(8,128)S(1)}, u32[]{:S(2)}, u32[]{:S(2)}) collective-permute-start(f32[192,512]{1,0:T(8,128)} %step.7.own_ref), channel_id=1, source_target_pairs={{0,8},{4,12},{8,0},{12,4},{1,9},{5,13},{9,1},{13,5},{2,10},{6,14},... | collective-permute-start | bytes 1179656 | tf_op jit(solution)/shard_map/ppermute | solution.py:231
  337.0 14.9 %collective-permute-start.24 = (f32[192,512]{1,0:T(8,128)}, f32[192,512]{1,0:T(8,128)S(1)}, u32[]{:S(2)}, u32[]{:S(2)}) collective-permute-start(f32[192,512]{1,0:T(8,128)} %step.7.own_ref), channel_id=1, source_target_pairs={{0,12},{4,0},{8,4},{12,8},{1,13},{5,1},{9,5},{13,9},{2,14},{6,2},{... | collective-permute-start | bytes 1179656 | tf_op jit(solution)/shard_map/ppermute | solution.py:231
  (18 other events, 75.2 us)
Sparse Core Ops, SparseCore 0:
  11.3 68.6 all-gather.7
  82.2 66.2 all-gather.5

commit v2 on v1

v2 whole, which is shorter than its diff:
```python
import functools

import jax
import jax.numpy as jnp
from jax import lax
from jax.experimental import pallas as pl
from jax.experimental.pallas import tpu as pltpu
from jax.sharding import Mesh
from jax.sharding import PartitionSpec as P


ROW = ("x", "core")
COL = ("y", "z")
SWAP = [(0, 1), (1, 0)]
HIGHEST = lax.Precision.HIGHEST


def full_dot(a, b):
    return jnp.dot(a, b, precision=HIGHEST, preferred_element_type=jnp.float32)


def dot_nt(a, b):
    return lax.dot_general(
        a, b, (((1,), (1,)), ((), ())), precision=HIGHEST, preferred_element_type=jnp.float32
    )


def inverse_into(tile_ref, out_ref):
    size, wide, small = 512, 128, 16
    parts = size // wide
    diag = jnp.concatenate(
        [tile_ref[wide * p : wide * (p + 1), wide * p : wide * (p + 1)] for p in range(parts)], axis=0
    )
    row = lax.broadcasted_iota(jnp.int32, (size, wide), 0)
    lane = lax.broadcasted_iota(jnp.int32, (size, wide), 1)
    local_row = row % wide
    lower = jnp.where(lane <= local_row, diag, 0.0)
    own = jnp.sum(jnp.where(lane == local_row, lower, 0.0), axis=1, keepdims=True)
    unit = lower / own
    inverse = jnp.where(lane == local_row, 1.0, 0.0)
    block_start = (local_row // small) * small
    inverse = inverse.reshape(size // small, small, wide)
    for i in range(small - 1):
        picked = jnp.where((lane == block_start + i) & (local_row > lane), unit, 0.0)
        weight = jnp.sum(picked, axis=1, keepdims=True).reshape(size // small, small, 1)
        inverse = inverse - weight * inverse[:, i : i + 1, :]
    inverse = inverse.reshape(size, wide)
    r1 = lax.broadcasted_iota(jnp.int32, (wide, wide), 0)
    c1 = lax.broadcasted_iota(jnp.int32, (wide, wide), 1)
    invs = [inverse[wide * p : wide * (p + 1)] for p in range(parts)]
    step = small
    while step < wide:
        keep = (r1 // (2 * step) == c1 // (2 * step)) & (r1 // step > c1 // step)
        offs = [jnp.where(keep, unit[wide * p : wide * (p + 1)], 0.0) for p in range(parts)]
        mids = [full_dot(offs[p], invs[p]) for p in range(parts)]
        invs = [invs[p] - full_dot(invs[p], mids[p]) for p in range(parts)]
        step *= 2
    out_ref[...] = jnp.zeros((size, size), jnp.float32)
    for p in range(parts):
        scale = jnp.broadcast_to(1.0 / own[wide * p : wide * (p + 1)], (wide, wide))
        as_row = jnp.sum(jnp.where(r1 == c1, scale, 0.0), axis=0, keepdims=True)
        out_ref[wide * p : wide * (p + 1), wide * p : wide * (p + 1)] = invs[p] * as_row
    step = wide
    while step < size:
        for s in range(0, size, 2 * step):
            top = out_ref[s : s + step, s : s + step]
            bottom = out_ref[s + step : s + 2 * step, s + step : s + 2 * step]
            between = tile_ref[s + step : s + 2 * step, s : s + step]
            out_ref[s + step : s + 2 * step, s : s + step] = -full_dot(bottom, full_dot(between, top))
        step *= 2


def by_core(place_ref, rows, put):
    core, y = place_ref[0], place_ref[1]
    for c in range(2):

        @pl.when(core == c)
        def _():
            for d in range(4):
                at = pl.multiple_of(lax.rem(y + (4 - d), 4) * rows, rows)
                put(d, pl.ds(at, rows), 256 * c, 256 * (1 - c))


def invert_body(place_ref, rows_ref, near_ref, far_ref, inverse_ref, first_ref, tile_ref):
    def put(d, at, here, there):
        tile_ref[at, here : here + 256] = near_ref[d]
        tile_ref[at, there : there + 256] = far_ref[d]

    by_core(place_ref, 128, put)
    inverse_into(tile_ref, inverse_ref)
    first_ref[...] = dot_nt(rows_ref[...], inverse_ref[...])


def gain_body(place_ref, inverse_ref, near_ref, far_ref, gain_ref, tile_ref):
    def put(d, at, here, there):
        for x in range(3):
            tile_ref[at, 512 * x + here : 512 * x + here + 256] = near_ref[d, x]
            tile_ref[at, 512 * x + there : 512 * x + there + 256] = far_ref[d, x]

    by_core(place_ref, 128, put)
    for x in range(3):
        gain_ref[x] = full_dot(inverse_ref[...], tile_ref[:, 512 * x : 512 * (x + 1)]).T


def in_vmem():
    return pl.BlockSpec(memory_space=pltpu.VMEM)


def in_smem():
    return pl.BlockSpec(memory_space=pltpu.SMEM)


def f32(*shape):
    return jax.ShapeDtypeStruct(shape, jnp.float32)


def invert(place, rows, near, far):
    return pl.pallas_call(
        invert_body,
        in_specs=[in_smem()] + [in_vmem()] * 3,
        out_specs=[in_vmem()] * 2,
        out_shape=[f32(512, 512), f32(192, 512)],
        scratch_shapes=[pltpu.VMEM((512, 512), jnp.float32)],
        name="invert",
    )(place, rows, near, far)


def gain(place, inverse, near, far):
    return pl.pallas_call(
        gain_body,
        in_specs=[in_smem()] + [in_vmem()] * 3,
        out_specs=in_vmem(),
        out_shape=f32(3, 512, 512),
        scratch_shapes=[pltpu.VMEM((512, 1536), jnp.float32)],
        name="gain",
    )(place, inverse, near, far)


def step_body(k, place_ref, left_ref, gain_ref, next_ref, out_ref):
    z = place_ref[2]

    @pl.when(z == k + 1)
    def _():
        out_ref[...] = left_ref[...] - full_dot(next_ref[...], gain_ref[0])

    @pl.when(z != k + 1)
    def _():
        out_ref[...] = left_ref[...]


def late_body(k, place_ref, own_ref, p1_ref, p2_ref, p3_ref, *rest):
    z = place_ref[2]
    mine_ref = rest[2] if len(rest) > 1 else rest[0]
    for d, ref in enumerate((own_ref, p1_ref, p2_ref, p3_ref)):

        @pl.when(z == (k + d) % 4)
        def _():
            mine_ref[...] = ref[...]

    if len(rest) > 1:
        left_ref, gain_ref, _, out_ref = rest

        @pl.when(z > k + 1)
        def _():
            out_ref[...] = left_ref[...] - full_dot(mine_ref[...], gain_ref[0])

        @pl.when(z <= k + 1)
        def _():
            out_ref[...] = left_ref[...]


def piece_spec():
    return pl.BlockSpec((192, 512), lambda i: (0, 0))


def gain_spec(k):
    return pl.BlockSpec((1, 512, 512), lambda i: (k, 0, 0))


def step(k, place, left, gains, arrived):
    return pl.pallas_call(
        functools.partial(step_body, k),
        grid=(1,),
        in_specs=[in_smem(), piece_spec(), gain_spec(k), piece_spec()],
        out_specs=piece_spec(),
        out_shape=f32(192, 512),
        name="step",
    )(place, left, gains, arrived)


def late(k, place, own, arrived, left=None, gains=None):
    more = left is not None
    return pl.pallas_call(
        functools.partial(late_body, k),
        grid=(1,),
        in_specs=[in_smem()] + [piece_spec()] * 4 + ([piece_spec(), gain_spec(k)] if more else []),
        out_specs=[piece_spec()] * (2 if more else 1),
        out_shape=[f32(192, 512)] * (2 if more else 1),
        name="late",
    )(place, own, *arrived, *((left, gains) if more else ()))


def pack_body(place_ref, own_ref, m1_ref, m2_ref, m3_ref, *rest):
    solved_ref, high_ref, low_ref = rest[-3:]
    core, y = place_ref[0], place_ref[1]
    for d, ref in enumerate((own_ref, m1_ref, m2_ref, m3_ref)):
        at = pl.multiple_of(lax.rem(y + (4 - d), 4) * 192, 192)
        value = ref[...]
        solved_ref[pl.ds(at, 192), :] = value
        left, right = value[:, :256], value[:, 256:]
        for half in range(2):
            part = jnp.where(core == half, left, right)
            high = part.astype(jnp.bfloat16)
            high_ref[half, pl.ds(at, 192), :] = high
            low_ref[half, pl.ds(at, 192), :] = (part - high.astype(jnp.float32)).astype(jnp.bfloat16)


def pack(k, place, pieces, into):
    operands = [place, *pieces]
    specs = [in_smem()] + [piece_spec()] * 4
    aliases = {}
    if into is not None:
        operands.append(into)
        specs.append(pl.BlockSpec(memory_space=pl.ANY))
        aliases = {5: 0}
    part = jax.ShapeDtypeStruct((2, 768, 256), jnp.bfloat16)
    part_spec = pl.BlockSpec((2, 768, 256), lambda i: (0, 0, 0))
    return pl.pallas_call(
        pack_body,
        grid=(1,),
        in_specs=specs,
        out_specs=[pl.BlockSpec((768, 512), lambda i: (0, k)), part_spec, part_spec],
        out_shape=[f32(768, 2048), part, part],
        input_output_aliases=aliases,
        name="pack",
    )(*operands)


def update_body(halves, first, count, block_ref, into_ref, *refs):
    xs, tiles = refs[: 2 * count], refs[2 * count : 2 * count + len(halves)]
    out_ref, high_ref, low_ref, xh_ref, xl_ref = refs[-5:]

    @pl.when(pl.program_id(0) == 0)
    def _():
        for p in range(count):
            for h in range(len(halves)):
                at = (p * len(halves) + h) * 256
                xh_ref[:, at : at + 256] = xs[2 * p][h]
                xl_ref[:, at : at + 256] = xs[2 * p + 1][h]

    block_id = block_ref[3] + pl.program_id(0) * 16
    for p in range(count):
        for h in range(len(halves)):
            at = (p * len(halves) + h) * 256
            part = jnp.where(first + p < block_id, tiles[h][p, 0], 0.0)
            high = part.astype(jnp.bfloat16)
            high_ref[:, at : at + 256] = high
            low_ref[:, at : at + 256] = (part - high.astype(jnp.float32)).astype(jnp.bfloat16)
    dims = (((1,), (1,)), ((), ()))
    high, low = high_ref[...], low_ref[...]
    total = lax.dot_general(xh_ref[...], high, dims, preferred_element_type=jnp.float32)
    total += lax.dot_general(xh_ref[...], low, dims, preferred_element_type=jnp.float32)
    total += lax.dot_general(xl_ref[...], high, dims, preferred_element_type=jnp.float32)
    out_ref[0] = into_ref[0] - total


def update(halves, first, place, into, xs, tiles, alias):
    count = len(xs)
    blocks, rows, width = into.shape
    big = pl.BlockSpec((1, rows, width), lambda l: (l, 0, 0))
    tile_spec = pl.BlockSpec((count, 1, width, 256), lambda l: (first // count, l, 0, 0))
    x_spec = pl.BlockSpec((len(halves), rows, 256), lambda l: (halves[0], 0, 0))
    depth = 256 * count * len(halves)
    return pl.pallas_call(
        functools.partial(update_body, halves, first, count),
        grid=(blocks,),
        in_specs=[in_smem(), big] + [x_spec] * (2 * count) + [tile_spec] * len(halves),
        out_specs=big,
        out_shape=f32(*into.shape),
        scratch_shapes=[pltpu.VMEM((width, depth), jnp.bfloat16)] * 2 + [pltpu.VMEM((rows, depth), jnp.bfloat16)] * 2,
        input_output_aliases={1: 0} if alias else {},
        compiler_params=pltpu.CompilerParams(vmem_limit_bytes=48 * 1024 * 1024),
        name="update",
    )(place, into, *[part for x in xs for part in x], *tiles)


def ring(shift):
    return [(i, (i + shift) % 4) for i in range(4)]


def over_z(value, k):
    return [lax.ppermute(value, "z", [(k, (k + d) % 4)]) for d in (1, 2, 3)]


def over_y(value):
    return [value] + [lax.ppermute(value, "y", ring(d)) for d in (1, 2, 3)]


def spread(piece, y):
    out = piece(0)
    moved = [lax.ppermute(piece(j), "y", [(0, j)]) for j in range(1, 4)]
    for j in range(1, 4):
        out = jnp.where(y == j, moved[j - 1], out)
    return out


def placed(matrix, factor):
    core, y, z = lax.axis_index("core"), lax.axis_index("y"), lax.axis_index("z")
    place = jnp.stack([core, y, z, y * 4 + z]).astype(jnp.int32)
    a = matrix.transpose(1, 0, 2)

    near = lax.all_gather(factor, "x")
    far = lax.ppermute(near, "core", SWAP)

    tile = spread(lambda j: factor[0, 128 * j : 128 * (j + 1)], y)
    rows = spread(lambda j: a[0, 192 * j : 192 * (j + 1)], y)
    tile = lax.all_gather(tile, "x")
    diag = jnp.stack(over_y(lax.dynamic_index_in_dim(tile, z, 0, keepdims=False)))
    diag_far = lax.ppermute(diag, "core", SWAP)
    inverse, left = invert(place, rows, diag, diag_far)
    pieces = over_y(tile[:3])
    off = jnp.stack(pieces)
    off_far = lax.ppermute(off, "core", SWAP)
    gains = gain(place, inverse, off, off_far)

    solved, parts, before = None, [], None

    def finish(k, mine, solved):
        pieces = over_y(mine)
        solved, high, low = pack(k, place, pieces, solved)
        parts.append((high, low))
        return solved

    for k in range(4):
        sent, moved = left, over_z(left, k)
        if k > 0:
            if k < 3:
                mine, left = late(k - 1, place, *before, left, gains)
            else:
                (mine,) = late(k - 1, place, *before)
            solved = finish(k - 1, mine, solved)
        if k < 3:
            left = step(k, place, left, gains, moved[0])
        before = (sent, moved)
    (mine,) = late(3, place, *before)
    solved = finish(3, mine, solved)

    out = update((0,), 0, place, a, parts[:3], [near], False)
    out = update((1,), 0, place, out, parts[:3], [far], True)
    out = update((0, 1), 3, place, out, parts[3:], [near, far], True)
    return out.transpose(1, 0, 2), solved


def solution(mesh):
    finer = Mesh(mesh.devices.reshape(4, 2, 4, 4), (*ROW, *COL))
    return jax.shard_map(
        placed,
        mesh=finer,
        in_specs=(P(ROW, None, COL), P(None, COL, ROW)),
        out_specs=(P(ROW, None, COL), P(ROW, None)),
        check_vma=False,
    )
```

time: 410 us -> 395 us (0.963)
  waiting for transfers between devices: 226 us -> 191 us
  Pallas kernels: 79.9 us -> 93.8 us
    ppermute x12, waiting for transfers between devices: 38.8 us -> 8.53 us  [over_z(): return [lax.ppermute(value, 'z', [(k, (k + d) % 4)]) for d in (1, 2, 3)]]
    pallas_call x7 -> x13, Pallas kernels: 61.5 us -> 87.1 us  [the longest x3 46.7 us: update(): pl.pallas_call(functools.partial(update_body, halves, first, count), grid...]
    ppermute x15 -> x18, waiting for transfers between devices: 34.2 us -> 53.4 us  [over_y(): return [value] + [lax.ppermute(value, 'y', ring(d)) for d in (1, 2, 3)]]
    ppermute x9, waiting for transfers between devices: 19.2 us -> 4.64 us  [the longest x6 4.63 us: spread(): moved = [lax.ppermute(piece(j), 'y', [(0, j)]) for j in range(1, 4)]]
    pallas_call x4 -> x3, Pallas kernels: 18.4 us -> 6.73 us  [step(): pl.pallas_call(functools.partial(step_body, k), grid=(1,), in_specs=[in_s...]
    all_gather x2 -> x1, waiting for transfers between devices: 133 us -> 123 us  [placed(): near = lax.all_gather(factor, 'x')]
    unnamed x56 -> x76, local copies, waits for them, and re-layouts: 3.57 us -> 9.22 us
    ppermute x15 -> x18, starting transfers between devices: 23.5 us -> 23.4 us  [over_y(): return [value] + [lax.ppermute(value, 'y', ring(d)) for d in (1, 2, 3)]]
  transfers between devices with their start and end apart: 38 -> 40, of which waited for: 18 -> 16; matrix products, arithmetic and copies ran while one was open for 1% -> 2% of each run, Pallas kernels for 15% -> 16%
where the time goes in v2:
time: 395 us; the launch traced here: 389 us
  waiting for transfers between devices  191 us (48%)
  Pallas kernels  93.8 us (24%)
  starting transfers between devices  63 us (16%)
  between operations  14.5 us (4%)
  local copies, waits for them, and re-layouts  11.6 us (3%)
  blocking collectives  10.6 us (3%)
  other arithmetic  4.59 us (1%)
    all_gather x1, waiting for transfers between devices, placed(): near = lax.all_gather(factor, 'x')  123 us
    ppermute x18, waiting for transfers between devices, over_y(): return [value] + [lax.ppermute(value, 'y', ring(d)) for d in (1, 2, 3)]  53.4 us
    pallas_call x3, Pallas kernels, update(): pl.pallas_call(functools.partial(update_body, halves, first, count), grid...  46.7 us
    ppermute x18, starting transfers between devices, over_y(): return [value] + [lax.ppermute(value, 'y', ring(d)) for d in (1, 2, 3)]  23.4 us
    ppermute x12, starting transfers between devices, over_z(): return [lax.ppermute(value, 'z', [(k, (k + d) % 4)]) for d in (1, 2, 3)]  16.3 us
    ppermute x6, starting transfers between devices, spread(): moved = [lax.ppermute(piece(j), 'y', [(0, j)]) for j in range(1, 4)]  16.3 us
    pallas_call x4, Pallas kernels, pack(): pl.pallas_call(pack_body, grid=(1,), in_specs=specs, out_specs=[pl.BlockS...  13.6 us
    all_gather x1, blocking collectives, placed(): tile = lax.all_gather(tile, 'x')  10.6 us
  transfers between devices with their start and end apart: 40, of which 16 were waited for; matrix products, arithmetic and copies ran while one was open for 2% of the time, Pallas kernels for 16%

profile of v2, /device:TPU:1, one launch (start us, length us, event | category | flops | bytes accessed | tf_op | source)
XLA Modules:
  0.0 388.8 jit_solution(15449309928045777448)
XLA Ops:
  7.9 123.3 %all-gather.4.cloned.1.call-done = f32[24,512,256]{2,1,0:T(8,128)} async-done(((f32[6,512,256]{2,1,0:T(8,128)}), f32[24,512,256]{2,1,0:T(8,128)}) %all-gather.4.cloned.1.call-update) | async-done | bytes 12582928 | tf_op jit(solution)/shard_map/all_gather | solution.py:312
  133.1 3.1 collective-permute-start.5
  136.2 2.2 collective-permute-start.4
  139.8 2.1 collective-permute-done.4
  143.5 10.6 %all-gather = f32[512,256]{1,0:T(8,128)S(1)} all-gather(f32[128,256]{1,0:T(8,128)S(1)} %fusion.4), channel_id=2, replica_groups=mesh['x'=4,'core'=2,'y'=4,'z'=4] {'x'}, dimensions={0}, use_global_device_ids=true | all-gather | bytes 655360 | tf_op jit(solution)/shard_map/all_gather | solution.py:317
  154.2 3.1 collective-permute-start.14
  158.2 1.7 collective-permute-start.15
  160.0 3.2 collective-permute-done.14
  163.3 11.1 %collective-permute-done.13 = f32[3,128,256]{2,1,0:T(8,128)S(1)} collective-permute-done((f32[3,128,256]{2,1,0:T(8,128)S(1)}, f32[3,128,256]{2,1,0:T(8,128)S(1)}, u32[]{:S(2)}, u32[]{:S(2)}) %collective-permute-start.13) | collective-permute-done | bytes 393248 | tf_op jit(solution)/shard_map/ppermute | solution.py:296
  176.4 3.8 collective-permute-start.16
  182.9 1.7 collective-permute-start.6
  184.6 9.1 %collective-permute-done.7 = f32[128,256]{1,0:T(8,128)S(1)} collective-permute-done((f32[128,256]{1,0:T(8,128)S(1)}, f32[128,256]{1,0:T(8,128)S(1)}, u32[]{:S(2)}, u32[]{:S(2)}) %collective-permute-start.7) | collective-permute-done | bytes 131104 | tf_op jit(solution)/shard_map/ppermute | solution.py:296
  193.6 6.4 %collective-permute-start.1 = (f32[192,512]{1,0:T(8,128)S(1)}, f32[192,512]{1,0:T(8,128)}, u32[]{:S(2)}, u32[]{:S(2)}) collective-permute-start(f32[192,512]{1,0:T(8,128)S(1)} %get-tuple-element.39), channel_id=1, source_target_pairs={{0,8},{1,9},{2,10},{3,11},{16,24},{17,25},{18,26},{19,27},{32,40},... | collective-permute-start | bytes 1179656 | tf_op jit(solution)/shard_map/ppermute | solution.py:301
  200.0 2.0 collective-permute-start
  202.9 2.3 collective-permute-start.9
  205.9 1.8 collective-permute-done
  207.7 1.9 fusion.2.rows_ref
  210.4 7.2 %invert.1 = (f32[512,512]{1,0:T(8,128)}, f32[192,512]{1,0:T(8,128)}) custom-call(s32[4]{0:T(128)} %pad_add_fusion.place_ref.block_ref, f32[192,512]{1,0:T(8,128)} %fusion.2.rows_ref, f32[4,128,256]{2,1,0:T(8,128)} %copy-done.11, f32[4,128,256]{2,1,0:T(8,128)} %copy-done.15), custom_call_target="tpu_custom_call" | custom-call | tf_op jit(solution)/shard_map/invert/pallas_call | solution.py:118
  217.6 3.2 collective-permute-start.10
  220.8 2.1 collective-permute-start.12
  224.2 9.6 %gain.1.gain_ref.rest_1_ = f32[3,512,512]{2,1,0:T(8,128)} custom-call(s32[4]{0:T(128)} %pad_add_fusion.place_ref.block_ref, f32[512,512]{1,0:T(8,128)} %get-tuple-element.21.inverse_ref, f32[4,3,128,256]{3,2,1,0:T(8,128)} %copy-done.9, f32[4,3,128,256]{3,2,1,0:T(8,128)} %collective-permute-done.16.far_ref), custom_call_target="tpu_custom_call" | custom-call | tf_op jit(solution)/shard_map/gain/pallas_call | solution.py:129
  234.6 2.2 step.3.rest_0_.own_ref
  239.1 2.8 late.4
  241.9 3.6 collective-permute-start.19
  249.0 2.2 step.4.rest_0_.own_ref
  257.1 2.8 late.5
  259.9 2.3 step.5.own_ref
  262.2 2.3 collective-permute-start.25
  264.5 5.3 %collective-permute-done.17.m1_ref = f32[192,512]{1,0:T(8,128)S(1)} collective-permute-done((f32[192,512]{1,0:T(8,128)S(1)}, f32[192,512]{1,0:T(8,128)S(1)}, u32[]{:S(2)}, u32[]{:S(2)}) %collective-permute-start.17) | collective-permute-done | bytes 393248 | tf_op jit(solution)/shard_map/ppermute | solution.py:296
  270.5 1.4 collective-permute-start.34
  272.7 1.5 collective-permute-start.33
  274.3 2.2 late.6.own_ref
  276.4 2.7 collective-permute-start.24
  279.1 2.7 collective-permute-start.31
  281.8 6.4 %collective-permute-done.33.p1_ref = f32[192,512]{1,0:T(8,128)} collective-permute-done((f32[192,512]{1,0:T(8,128)}, f32[192,512]{1,0:T(8,128)}, u32[]{:S(2)}, u32[]{:S(2)}) %collective-permute-start.33) | collective-permute-done | bytes 393248 | tf_op jit(solution)/shard_map/ppermute | solution.py:292
  288.2 2.6 collective-permute-start.30
  290.8 2.2 late.7.own_ref
  293.0 4.0 %collective-permute-done.23.m1_ref = f32[192,512]{1,0:T(8,128)S(1)} collective-permute-done((f32[192,512]{1,0:T(8,128)S(1)}, f32[192,512]{1,0:T(8,128)S(1)}, u32[]{:S(2)}, u32[]{:S(2)}) %collective-permute-start.23) | collective-permute-done | bytes 393248 | tf_op jit(solution)/shard_map/ppermute | solution.py:296
  297.1 4.0 %collective-permute-done.30.m2_ref = f32[192,512]{1,0:T(8,128)S(1)} collective-permute-done((f32[192,512]{1,0:T(8,128)}, f32[192,512]{1,0:T(8,128)S(1)}, u32[]{:S(2)}, u32[]{:S(2)}) %collective-permute-start.30) | collective-permute-done | bytes 393248 | tf_op jit(solution)/shard_map/ppermute | solution.py:296
  301.1 3.4 pack.4
  304.5 3.3 pack.5
  307.9 6.0 %collective-permute-done.29.m1_ref = f32[192,512]{1,0:T(8,128)S(1)} collective-permute-done((f32[192,512]{1,0:T(8,128)}, f32[192,512]{1,0:T(8,128)S(1)}, u32[]{:S(2)}, u32[]{:S(2)}) %collective-permute-start.29) | collective-permute-done | bytes 393248 | tf_op jit(solution)/shard_map/ppermute | solution.py:296
  314.6 3.4 pack.6
  318.0 10.5 %collective-permute-done.36.m1_ref = f32[192,512]{1,0:T(8,128)S(1)} collective-permute-done((f32[192,512]{1,0:T(8,128)}, f32[192,512]{1,0:T(8,128)S(1)}, u32[]{:S(2)}, u32[]{:S(2)}) %collective-permute-start.36) | collective-permute-done | bytes 393248 | tf_op jit(solution)/shard_map/ppermute | solution.py:296
  329.4 3.5 pack.7
  335.2 16.5 %update.3.into_ref = f32[6,768,512]{2,1,0:T(8,128)} custom-call(s32[4]{0:T(128)S(1)} %copy-done.8, f32[6,768,512]{2,1,0:T(8,128)} %bitcast.50, bf16[2,768,256]{2,1,0:T(8,128)(2,1)S(1)} %copy-done, bf16[2,768,256]{2,1,0:T(8,128)(2,1)S(1)} %copy-done.1, bf16[2,768,256]{2,1,0:T(8,128)(2,1)S(1)} %copy-done.2, bf16[2,768,256]{2,1,0:T(8,128)(2,1)S(1)} %copy-done.3, ...), custom_call_target="tpu_custom_call" | custom-call | tf_op jit(solution)/shard_map/update/pallas_call | solution.py:274
  351.7 16.6 %update.4.into_ref = f32[6,768,512]{2,1,0:T(8,128)} custom-call(s32[4]{0:T(128)S(1)} %copy-done.8, f32[6,768,512]{2,1,0:T(8,128)} %update.3.into_ref, bf16[2,768,256]{2,1,0:T(8,128)(2,1)S(1)} %copy-done, bf16[2,768,256]{2,1,0:T(8,128)(2,1)S(1)} %copy-done.1, bf16[2,768,256]{2,1,0:T(8,128)(2,1)S(1)} %copy-done.2, ...), custom_call_target="tpu_custom_call", output_to_operand_aliasing={{}: (1, {})} | custom-call | tf_op jit(solution)/shard_map/update/pallas_call | solution.py:274
  368.3 13.6 %update.5 = f32[6,768,512]{2,1,0:T(8,128)} custom-call(s32[4]{0:T(128)S(1)} %copy-done.8, f32[6,768,512]{2,1,0:T(8,128)} %update.4.into_ref, bf16[2,768,256]{2,1,0:T(8,128)(2,1)S(1)} %copy-done.6, bf16[2,768,256]{2,1,0:T(8,128)(2,1)S(1)} %copy-done.7, f32[4,6,512,256]{3,2,1,0:T(8,128)} %bitcast.47, ...), custom_call_target="tpu_custom_call", output_to_operand_aliasing={{}: (1, {})} | custom-call | tf_op jit(solution)/shard_map/update/pallas_call | solution.py:274
  (136 shorter events, 32.6 us)
Async XLA Ops:
  7.2 124.1 %all-gather.4.cloned.1.call-start = ((), (), s32[]{:S(2)}) async-start(), calls=%async_computation | async-start | bytes 15728640 | tf_op jit(solution)/shard_map/all_gather | solution.py:312
  131.2 220.5 %collective-permute-start.32 = (f32[4,6,512,256]{3,2,1,0:T(8,128)}, f32[4,6,512,256]{3,2,1,0:T(8,128)}, u32[]{:S(2)}, u32[]{:S(2)}) collective-permute-start(f32[4,6,512,256]{3,2,1,0:T(8,128)} %bitcast.45), channel_id=1, source_target_pairs={{0,16},{16,0},{1,17},{17,1},{2,18},{18,2},{3,19},{19,3},{4,20},{20... | collective-permute-start | bytes 37748744 | tf_op jit(solution)/shard_map/ppermute | solution.py:313
  133.1 6.6 %collective-permute-start.5 = (f32[128,256]{1,0:T(8,128)S(1)}, f32[128,256]{1,0:T(8,128)S(1)}, u32[]{:S(2)}, u32[]{:S(2)}) collective-permute-start(f32[128,256]{1,0:T(8,128)S(1)} %get-tuple-element.41), channel_id=1, source_target_pairs={{0,4},{1,5},{2,6},{3,7},{16,20},{17,21},{18,22},{19,23},{32,36},{3... | collective-permute-start | bytes 393224 | tf_op jit(solution)/shard_map/ppermute | solution.py:301
  136.2 5.6 %collective-permute-start.4 = (f32[128,256]{1,0:T(8,128)S(1)}, f32[128,256]{1,0:T(8,128)S(1)}, u32[]{:S(2)}, u32[]{:S(2)}) collective-permute-start(f32[128,256]{1,0:T(8,128)S(1)} %get-tuple-element.42), channel_id=1, source_target_pairs={{0,8},{1,9},{2,10},{3,11},{16,24},{17,25},{18,26},{19,27},{32,40},... | collective-permute-start | bytes 393224 | tf_op jit(solution)/shard_map/ppermute | solution.py:301
  138.4 4.1 %collective-permute-start.3 = (f32[128,256]{1,0:T(8,128)S(1)}, f32[128,256]{1,0:T(8,128)S(1)}, u32[]{:S(2)}, u32[]{:S(2)}) collective-permute-start(f32[128,256]{1,0:T(8,128)S(1)} %get-tuple-element.43), channel_id=1, source_target_pairs={{0,12},{1,13},{2,14},{3,15},{16,28},{17,29},{18,30},{19,31},{32,44... | collective-permute-start | bytes 393224 | tf_op jit(solution)/shard_map/ppermute | solution.py:301
  154.2 9.1 %collective-permute-start.14 = (f32[3,128,256]{2,1,0:T(8,128)S(1)}, f32[3,128,256]{2,1,0:T(8,128)S(1)}, u32[]{:S(2)}, u32[]{:S(2)}) collective-permute-start(f32[3,128,256]{2,1,0:T(8,128)S(1)} %bitcast.53), channel_id=1, source_target_pairs={{0,8},{4,12},{8,0},{12,4},{1,9},{5,13},{9,1},{13,5},{2,10},{6,14},... | collective-permute-start | bytes 1179656 | tf_op jit(solution)/shard_map/ppermute | solution.py:296
  157.3 17.1 %collective-permute-start.13 = (f32[3,128,256]{2,1,0:T(8,128)S(1)}, f32[3,128,256]{2,1,0:T(8,128)S(1)}, u32[]{:S(2)}, u32[]{:S(2)}) collective-permute-start(f32[3,128,256]{2,1,0:T(8,128)S(1)} %bitcast.54), channel_id=1, source_target_pairs={{0,4},{4,8},{8,12},{12,0},{1,5},{5,9},{9,13},{13,1},{2,6},{6,10},{... | collective-permute-start | bytes 1179656 | tf_op jit(solution)/shard_map/ppermute | solution.py:296
  158.2 16.2 %collective-permute-start.15 = (f32[3,128,256]{2,1,0:T(8,128)S(1)}, f32[3,128,256]{2,1,0:T(8,128)S(1)}, u32[]{:S(2)}, u32[]{:S(2)}) collective-permute-start(f32[3,128,256]{2,1,0:T(8,128)S(1)} %bitcast.55), channel_id=1, source_target_pairs={{0,12},{4,0},{8,4},{12,8},{1,13},{5,1},{9,5},{13,9},{2,14},{6,2},{... | collective-permute-start | bytes 1179656 | tf_op jit(solution)/shard_map/ppermute | solution.py:296
  160.0 22.9 %collective-permute-start.8 = (f32[128,256]{1,0:T(8,128)S(1)}, f32[128,256]{1,0:T(8,128)S(1)}, u32[]{:S(2)}, u32[]{:S(2)}) collective-permute-start(f32[128,256]{1,0:T(8,128)S(1)} %fusion.5), channel_id=1, source_target_pairs={{0,12},{4,0},{8,4},{12,8},{1,13},{5,1},{9,5},{13,9},{2,14},{6,2},{... | collective-permute-start | bytes 393224 | tf_op jit(solution)/shard_map/ppermute | solution.py:296
  176.3 41.2 %copy-start.9 = (f32[4,3,128,256]{3,2,1,0:T(8,128)}, f32[4,3,128,256]{3,2,1,0:T(8,128)S(1)}, u32[]{:S(2)}) copy-start(f32[4,3,128,256]{3,2,1,0:T(8,128)S(1)} %pad_maximum_fusion.near_ref) | copy-start | bytes 4718596
  176.4 47.8 %collective-permute-start.16 = (f32[4,3,128,256]{3,2,1,0:T(8,128)S(1)}, f32[4,3,128,256]{3,2,1,0:T(8,128)}, u32[]{:S(2)}, u32[]{:S(2)}) collective-permute-start(f32[4,3,128,256]{3,2,1,0:T(8,128)S(1)} %pad_maximum_fusion.near_ref), channel_id=1, source_target_pairs={{0,16},{16,0},{1,17},{17,1},{2,18},{18,2},{3,19},{19,3},{4,20},{20... | collective-permute-start | bytes 4718600 | tf_op jit(solution)/shard_map/ppermute | solution.py:323
  181.5 20.7 %collective-permute-start.2 = (f32[192,512]{1,0:T(8,128)S(1)}, f32[192,512]{1,0:T(8,128)S(1)}, u32[]{:S(2)}, u32[]{:S(2)}) collective-permute-start(f32[192,512]{1,0:T(8,128)S(1)} %get-tuple-element.38), channel_id=1, source_target_pairs={{0,4},{1,5},{2,6},{3,7},{16,20},{17,21},{18,22},{19,23},{32,36},{3... | collective-permute-start | bytes 1179656 | tf_op jit(solution)/shard_map/ppermute | solution.py:301
  182.8 10.9 %collective-permute-start.7 = (f32[128,256]{1,0:T(8,128)S(1)}, f32[128,256]{1,0:T(8,128)S(1)}, u32[]{:S(2)}, u32[]{:S(2)}) collective-permute-start(f32[128,256]{1,0:T(8,128)S(1)} %fusion.5), channel_id=1, source_target_pairs={{0,8},{4,12},{8,0},{12,4},{1,9},{5,13},{9,1},{13,5},{2,10},{6,14},... | collective-permute-start | bytes 393224 | tf_op jit(solution)/shard_map/ppermute | solution.py:296
  182.9 17.1 %collective-permute-start.6 = (f32[128,256]{1,0:T(8,128)S(1)}, f32[128,256]{1,0:T(8,128)S(1)}, u32[]{:S(2)}, u32[]{:S(2)}) collective-permute-start(f32[128,256]{1,0:T(8,128)S(1)} %fusion.5), channel_id=1, source_target_pairs={{0,4},{4,8},{8,12},{12,0},{1,5},{5,9},{9,13},{13,1},{2,6},{6,10},{... | collective-permute-start | bytes 393224 | tf_op jit(solution)/shard_map/ppermute | solution.py:296
  193.6 12.2 %collective-permute-start.1 = (f32[192,512]{1,0:T(8,128)S(1)}, f32[192,512]{1,0:T(8,128)}, u32[]{:S(2)}, u32[]{:S(2)}) collective-permute-start(f32[192,512]{1,0:T(8,128)S(1)} %get-tuple-element.39), channel_id=1, source_target_pairs={{0,8},{1,9},{2,10},{3,11},{16,24},{17,25},{18,26},{19,27},{32,40},... | collective-permute-start | bytes 1179656 | tf_op jit(solution)/shard_map/ppermute | solution.py:301
  200.0 7.7 %collective-permute-start = (f32[192,512]{1,0:T(8,128)S(1)}, f32[192,512]{1,0:T(8,128)}, u32[]{:S(2)}, u32[]{:S(2)}) collective-permute-start(f32[192,512]{1,0:T(8,128)S(1)} %get-tuple-element.40), channel_id=1, source_target_pairs={{0,12},{1,13},{2,14},{3,15},{16,28},{17,29},{18,30},{19,31},{32,44... | collective-permute-start | bytes 1179656 | tf_op jit(solution)/shard_map/ppermute | solution.py:301
  202.9 6.7 %collective-permute-start.9 = (f32[4,128,256]{2,1,0:T(8,128)S(1)}, f32[4,128,256]{2,1,0:T(8,128)S(1)}, u32[]{:S(2)}, u32[]{:S(2)}) collective-permute-start(f32[4,128,256]{2,1,0:T(8,128)S(1)} %pad_maximum_fusion.1.near_ref), channel_id=1, source_target_pairs={{0,16},{16,0},{1,17},{17,1},{2,18},{18,2},{3,19},{19,3},{4,20},{20... | collective-permute-start | bytes 1572872 | tf_op jit(solution)/shard_map/ppermute | solution.py:319
  217.6 16.2 %collective-permute-start.10 = (f32[192,512]{1,0:T(8,128)}, f32[192,512]{1,0:T(8,128)S(1)}, u32[]{:S(2)}, u32[]{:S(2)}) collective-permute-start(f32[192,512]{1,0:T(8,128)} %get-tuple-element.20.left_ref.own_ref), channel_id=1, source_target_pairs={{0,1},{4,5},{8,9},{12,13},{16,17},{20,21},{24,25},{28,29},{32,33},... | collective-permute-start | bytes 1179656 | tf_op jit(solution)/shard_map/ppermute | solution.py:292
  220.8 16.8 %collective-permute-start.12 = (f32[192,512]{1,0:T(8,128)}, f32[192,512]{1,0:T(8,128)S(1)}, u32[]{:S(2)}, u32[]{:S(2)}) collective-permute-start(f32[192,512]{1,0:T(8,128)} %get-tuple-element.20.left_ref.own_ref), channel_id=1, source_target_pairs={{0,3},{4,7},{8,11},{12,15},{16,19},{20,23},{24,27},{28,31},{32,35}... | collective-permute-start | bytes 1179656 | tf_op jit(solution)/shard_map/ppermute | solution.py:292
  222.9 14.8 %collective-permute-start.11 = (f32[192,512]{1,0:T(8,128)}, f32[192,512]{1,0:T(8,128)S(1)}, u32[]{:S(2)}, u32[]{:S(2)}) collective-permute-start(f32[192,512]{1,0:T(8,128)} %get-tuple-element.20.left_ref.own_ref), channel_id=1, source_target_pairs={{0,2},{4,6},{8,10},{12,14},{16,18},{20,22},{24,26},{28,30},{32,34}... | collective-permute-start | bytes 1179656 | tf_op jit(solution)/shard_map/ppermute | solution.py:292
  236.8 11.5 %collective-permute-start.20 = (f32[192,512]{1,0:T(8,128)}, f32[192,512]{1,0:T(8,128)S(1)}, u32[]{:S(2)}, u32[]{:S(2)}) collective-permute-start(f32[192,512]{1,0:T(8,128)} %step.3.rest_0_.own_ref), channel_id=1, source_target_pairs={{1,2},{5,6},{9,10},{13,14},{17,18},{21,22},{25,26},{29,30},{33,34}... | collective-permute-start | bytes 1179656 | tf_op jit(solution)/shard_map/ppermute | solution.py:292
  241.9 10.0 %collective-permute-start.19 = (f32[192,512]{1,0:T(8,128)}, f32[192,512]{1,0:T(8,128)S(1)}, u32[]{:S(2)}, u32[]{:S(2)}) collective-permute-start(f32[192,512]{1,0:T(8,128)} %get-tuple-element.22.own_ref), channel_id=1, source_target_pairs={{0,12},{4,0},{8,4},{12,8},{1,13},{5,1},{9,5},{13,9},{2,14},{6,2},{... | collective-permute-start | bytes 1179656 | tf_op jit(solution)/shard_map/ppermute | solution.py:296
  245.6 9.1 %collective-permute-start.22 = (f32[192,512]{1,0:T(8,128)S(1)}, f32[192,512]{1,0:T(8,128)S(1)}, u32[]{:S(2)}, u32[]{:S(2)}) collective-permute-start(f32[192,512]{1,0:T(8,128)S(1)} %copy-done.10), channel_id=1, source_target_pairs={{1,0},{5,4},{9,8},{13,12},{17,16},{21,20},{25,24},{29,28},{33,32},... | collective-permute-start | bytes 1179656 | tf_op jit(solution)/shard_map/ppermute | solution.py:292
  246.9 8.2 %collective-permute-start.21 = (f32[192,512]{1,0:T(8,128)S(1)}, f32[192,512]{1,0:T(8,128)}, u32[]{:S(2)}, u32[]{:S(2)}) collective-permute-start(f32[192,512]{1,0:T(8,128)S(1)} %copy-done.10), channel_id=1, source_target_pairs={{1,3},{5,7},{9,11},{13,15},{17,19},{21,23},{25,27},{29,31},{33,35}... | collective-permute-start | bytes 1179656 | tf_op jit(solution)/shard_map/ppermute | solution.py:292
  251.3 4.5 %collective-permute-start.26 = (f32[192,512]{1,0:T(8,128)}, f32[192,512]{1,0:T(8,128)S(1)}, u32[]{:S(2)}, u32[]{:S(2)}) collective-permute-start(f32[192,512]{1,0:T(8,128)} %step.4.rest_0_.own_ref), channel_id=1, source_target_pairs={{2,3},{6,7},{10,11},{14,15},{18,19},{22,23},{26,27},{30,31},{34,35... | collective-permute-start | bytes 1179656 | tf_op jit(solution)/shard_map/ppermute | solution.py:292
  252.0 10.2 %collective-permute-start.18 = (f32[192,512]{1,0:T(8,128)S(1)}, f32[192,512]{1,0:T(8,128)S(1)}, u32[]{:S(2)}, u32[]{:S(2)}) collective-permute-start(f32[192,512]{1,0:T(8,128)S(1)} %copy-done.27), channel_id=1, source_target_pairs={{0,8},{4,12},{8,0},{12,4},{1,9},{5,13},{9,1},{13,5},{2,10},{6,14},... | collective-permute-start | bytes 1179656 | tf_op jit(solution)/shard_map/ppermute | solution.py:296
  254.7 15.2 %collective-permute-start.17 = (f32[192,512]{1,0:T(8,128)S(1)}, f32[192,512]{1,0:T(8,128)S(1)}, u32[]{:S(2)}, u32[]{:S(2)}) collective-permute-start(f32[192,512]{1,0:T(8,128)S(1)} %copy-done.27), channel_id=1, source_target_pairs={{0,4},{4,8},{8,12},{12,0},{1,5},{5,9},{9,13},{13,1},{2,6},{6,10},{... | collective-permute-start | bytes 1179656 | tf_op jit(solution)/shard_map/ppermute | solution.py:296
  255.1 15.5 %collective-permute-start.28 = (f32[192,512]{1,0:T(8,128)}, f32[192,512]{1,0:T(8,128)S(1)}, u32[]{:S(2)}, u32[]{:S(2)}) collective-permute-start(f32[192,512]{1,0:T(8,128)} %step.4.rest_0_.own_ref), channel_id=1, source_target_pairs={{2,1},{6,5},{10,9},{14,13},{18,17},{22,21},{26,25},{30,29},{34,33}... | collective-permute-start | bytes 1179656 | tf_op jit(solution)/shard_map/ppermute | solution.py:292
  255.8 17.0 %collective-permute-start.27 = (f32[192,512]{1,0:T(8,128)}, f32[192,512]{1,0:T(8,128)S(1)}, u32[]{:S(2)}, u32[]{:S(2)}) collective-permute-start(f32[192,512]{1,0:T(8,128)} %step.4.rest_0_.own_ref), channel_id=1, source_target_pairs={{2,0},{6,4},{10,8},{14,12},{18,16},{22,20},{26,24},{30,28},{34,32}... | collective-permute-start | bytes 1179656 | tf_op jit(solution)/shard_map/ppermute | solution.py:292
  262.2 14.2 %copy-start.29 = (f32[192,512]{1,0:T(8,128)}, f32[192,512]{1,0:T(8,128)S(1)}, u32[]{:S(2)}) copy-start(f32[192,512]{1,0:T(8,128)S(1)} %collective-permute-done.18.m2_ref) | copy-start | bytes 1179652
  262.2 14.2 %collective-permute-start.25 = (f32[192,512]{1,0:T(8,128)S(1)}, f32[192,512]{1,0:T(8,128)S(1)}, u32[]{:S(2)}, u32[]{:S(2)}) collective-permute-start(f32[192,512]{1,0:T(8,128)S(1)} %copy-done.16), channel_id=1, source_target_pairs={{0,12},{4,0},{8,4},{12,8},{1,13},{5,1},{9,5},{13,9},{2,14},{6,2},{... | collective-permute-start | bytes 1179656 | tf_op jit(solution)/shard_map/ppermute | solution.py:296
  269.8 11.9 %copy-start.30 = (f32[192,512]{1,0:T(8,128)}, f32[192,512]{1,0:T(8,128)S(1)}, u32[]{:S(2)}) copy-start(f32[192,512]{1,0:T(8,128)S(1)} %collective-permute-done.17.m1_ref) | copy-start | bytes 1179652
  269.8 9.3 %collective-permute-start.35 = (f32[192,512]{1,0:T(8,128)}, f32[192,512]{1,0:T(8,128)S(1)}, u32[]{:S(2)}, u32[]{:S(2)}) collective-permute-start(f32[192,512]{1,0:T(8,128)} %step.5.own_ref), channel_id=1, source_target_pairs={{3,2},{7,6},{11,10},{15,14},{19,18},{23,22},{27,26},{31,30},{35,34... | collective-permute-start | bytes 1179656 | tf_op jit(solution)/shard_map/ppermute | solution.py:292
  270.5 8.6 %collective-permute-start.34 = (f32[192,512]{1,0:T(8,128)}, f32[192,512]{1,0:T(8,128)}, u32[]{:S(2)}, u32[]{:S(2)}) collective-permute-start(f32[192,512]{1,0:T(8,128)} %step.5.own_ref), channel_id=1, source_target_pairs={{3,1},{7,5},{11,9},{15,13},{19,17},{23,21},{27,25},{31,29},{35,33}... | collective-permute-start | bytes 1179656 | tf_op jit(solution)/shard_map/ppermute | solution.py:292
  272.7 15.5 %collective-permute-start.33 = (f32[192,512]{1,0:T(8,128)}, f32[192,512]{1,0:T(8,128)}, u32[]{:S(2)}, u32[]{:S(2)}) collective-permute-start(f32[192,512]{1,0:T(8,128)} %step.5.own_ref), channel_id=1, source_target_pairs={{3,0},{7,4},{11,8},{15,12},{19,16},{23,20},{27,24},{31,28},{35,32}... | collective-permute-start | bytes 1179656 | tf_op jit(solution)/shard_map/ppermute | solution.py:292
  276.4 28.1 %copy-start.17 = (f32[192,512]{1,0:T(8,128)}, f32[192,512]{1,0:T(8,128)S(1)}, u32[]{:S(2)}) copy-start(f32[192,512]{1,0:T(8,128)S(1)} %collective-permute-done.25.m3_ref) | copy-start | bytes 1179652
  276.4 16.5 %collective-permute-start.24 = (f32[192,512]{1,0:T(8,128)S(1)}, f32[192,512]{1,0:T(8,128)S(1)}, u32[]{:S(2)}, u32[]{:S(2)}) collective-permute-start(f32[192,512]{1,0:T(8,128)S(1)} %copy-done.16), channel_id=1, source_target_pairs={{0,8},{4,12},{8,0},{12,4},{1,9},{5,13},{9,1},{13,5},{2,10},{6,14},... | collective-permute-start | bytes 1179656 | tf_op jit(solution)/shard_map/ppermute | solution.py:296
  279.1 11.7 %copy-start.32 = (f32[192,512]{1,0:T(8,128)}, f32[192,512]{1,0:T(8,128)S(1)}, u32[]{:S(2)}) copy-start(f32[192,512]{1,0:T(8,128)S(1)} %collective-permute-done.35.p3_ref) | copy-start | bytes 1179652
  279.1 17.9 %collective-permute-start.23 = (f32[192,512]{1,0:T(8,128)S(1)}, f32[192,512]{1,0:T(8,128)S(1)}, u32[]{:S(2)}, u32[]{:S(2)}) collective-permute-start(f32[192,512]{1,0:T(8,128)S(1)} %copy-done.16), channel_id=1, source_target_pairs={{0,4},{4,8},{8,12},{12,0},{1,5},{5,9},{9,13},{13,1},{2,6},{6,10},{... | collective-permute-start | bytes 1179656 | tf_op jit(solution)/shard_map/ppermute | solution.py:296
  279.1 17.9 %collective-permute-start.31 = (f32[192,512]{1,0:T(8,128)}, f32[192,512]{1,0:T(8,128)S(1)}, u32[]{:S(2)}, u32[]{:S(2)}) collective-permute-start(f32[192,512]{1,0:T(8,128)} %late.6.own_ref), channel_id=1, source_target_pairs={{0,12},{4,0},{8,4},{12,8},{1,13},{5,1},{9,5},{13,9},{2,14},{6,2},{... | collective-permute-start | bytes 1179656 | tf_op jit(solution)/shard_map/ppermute | solution.py:296
  288.2 12.9 %collective-permute-start.30 = (f32[192,512]{1,0:T(8,128)}, f32[192,512]{1,0:T(8,128)S(1)}, u32[]{:S(2)}, u32[]{:S(2)}) collective-permute-start(f32[192,512]{1,0:T(8,128)} %late.6.own_ref), channel_id=1, source_target_pairs={{0,8},{4,12},{8,0},{12,4},{1,9},{5,13},{9,1},{13,5},{2,10},{6,14},... | collective-permute-start | bytes 1179656 | tf_op jit(solution)/shard_map/ppermute | solution.py:296
  292.9 11.6 %copy-start.18 = (f32[192,512]{1,0:T(8,128)}, f32[192,512]{1,0:T(8,128)S(1)}, u32[]{:S(2)}) copy-start(f32[192,512]{1,0:T(8,128)S(1)} %collective-permute-done.24.m2_ref) | copy-start | bytes 1179652
  292.9 20.9 %collective-permute-start.29 = (f32[192,512]{1,0:T(8,128)}, f32[192,512]{1,0:T(8,128)S(1)}, u32[]{:S(2)}, u32[]{:S(2)}) collective-permute-start(f32[192,512]{1,0:T(8,128)} %late.6.own_ref), channel_id=1, source_target_pairs={{0,4},{4,8},{8,12},{12,0},{1,5},{5,9},{9,13},{13,1},{2,6},{6,10},{... | collective-permute-start | bytes 1179656 | tf_op jit(solution)/shard_map/ppermute | solution.py:296
  297.0 21.0 %collective-permute-start.38 = (f32[192,512]{1,0:T(8,128)}, f32[192,512]{1,0:T(8,128)S(1)}, u32[]{:S(2)}, u32[]{:S(2)}) collective-permute-start(f32[192,512]{1,0:T(8,128)} %late.7.own_ref), channel_id=1, source_target_pairs={{0,12},{4,0},{8,4},{12,8},{1,13},{5,1},{9,5},{13,9},{2,14},{6,2},{... | collective-permute-start | bytes 1179656 | tf_op jit(solution)/shard_map/ppermute | solution.py:296
  297.0 21.0 %collective-permute-start.37 = (f32[192,512]{1,0:T(8,128)}, f32[192,512]{1,0:T(8,128)S(1)}, u32[]{:S(2)}, u32[]{:S(2)}) collective-permute-start(f32[192,512]{1,0:T(8,128)} %late.7.own_ref), channel_id=1, source_target_pairs={{0,8},{4,12},{8,0},{12,4},{1,9},{5,13},{9,1},{13,5},{2,10},{6,14},... | collective-permute-start | bytes 1179656 | tf_op jit(solution)/shard_map/ppermute | solution.py:296
  301.1 27.5 %collective-permute-start.36 = (f32[192,512]{1,0:T(8,128)}, f32[192,512]{1,0:T(8,128)S(1)}, u32[]{:S(2)}, u32[]{:S(2)}) collective-permute-start(f32[192,512]{1,0:T(8,128)} %late.7.own_ref), channel_id=1, source_target_pairs={{0,4},{4,8},{8,12},{12,0},{1,5},{5,9},{9,13},{13,1},{2,6},{6,10},{... | collective-permute-start | bytes 1179656 | tf_op jit(solution)/shard_map/ppermute | solution.py:296
  351.7 16.7 %copy-start.6 = (bf16[2,768,256]{2,1,0:T(8,128)(2,1)S(1)}, bf16[2,768,256]{2,1,0:T(8,128)(2,1)}, u32[]{:S(2)}) copy-start(bf16[2,768,256]{2,1,0:T(8,128)(2,1)} %get-tuple-element.35.refs_0_) | copy-start | bytes 2359300
  351.7 16.7 %copy-start.7 = (bf16[2,768,256]{2,1,0:T(8,128)(2,1)S(1)}, bf16[2,768,256]{2,1,0:T(8,128)(2,1)}, u32[]{:S(2)}) copy-start(bf16[2,768,256]{2,1,0:T(8,128)(2,1)} %get-tuple-element.36.refs_1_) | copy-start | bytes 2359300
  (30 other events, 124.5 us)
Sparse Core Ops, SparseCore 0:
  9.6 121.5 all-gather.3

commit v3 on v2

--- a/solution.py
+++ b/solution.py
@@ -88,18 +88,16 @@
 
     by_core(place_ref, 128, put)
     inverse_into(tile_ref, inverse_ref)
-    first_ref[...] = dot_nt(rows_ref[...], inverse_ref[...])
-
-
-def gain_body(place_ref, inverse_ref, near_ref, far_ref, gain_ref, tile_ref):
+    inverse_ref[...] = inverse_ref[...].T
+    first_ref[...] = full_dot(rows_ref[...], inverse_ref[...])
+
+
+def tile_into(place_ref, near_ref, far_ref, tile_ref):
     def put(d, at, here, there):
-        for x in range(3):
-            tile_ref[at, 512 * x + here : 512 * x + here + 256] = near_ref[d, x]
-            tile_ref[at, 512 * x + there : 512 * x + there + 256] = far_ref[d, x]
+        tile_ref[at, here : here + 256] = near_ref[d, 0]
+        tile_ref[at, there : there + 256] = far_ref[d, 0]
 
     by_core(place_ref, 128, put)
-    for x in range(3):
-        gain_ref[x] = full_dot(inverse_ref[...], tile_ref[:, 512 * x : 512 * (x + 1)]).T
 
 
 def in_vmem():
@@ -125,32 +123,23 @@
     )(place, rows, near, far)
 
 
-def gain(place, inverse, near, far):
-    return pl.pallas_call(
-        gain_body,
-        in_specs=[in_smem()] + [in_vmem()] * 3,
-        out_specs=in_vmem(),
-        out_shape=f32(3, 512, 512),
-        scratch_shapes=[pltpu.VMEM((512, 1536), jnp.float32)],
-        name="gain",
-    )(place, inverse, near, far)
-
-
-def step_body(k, place_ref, left_ref, gain_ref, next_ref, out_ref):
+def step_body(k, place_ref, left_ref, near_ref, far_ref, inverse_ref, next_ref, out_ref, tile_ref):
     z = place_ref[2]
 
     @pl.when(z == k + 1)
     def _():
-        out_ref[...] = left_ref[...] - full_dot(next_ref[...], gain_ref[0])
+        tile_into(place_ref, near_ref, far_ref, tile_ref)
+        rest = left_ref[...] - dot_nt(next_ref[...], tile_ref[...])
+        out_ref[...] = full_dot(rest, inverse_ref[...])
 
     @pl.when(z != k + 1)
     def _():
-        out_ref[...] = left_ref[...]
+        out_ref[...] = jnp.zeros((192, 512), jnp.float32)
 
 
 def late_body(k, place_ref, own_ref, p1_ref, p2_ref, p3_ref, *rest):
     z = place_ref[2]
-    mine_ref = rest[2] if len(rest) > 1 else rest[0]
+    mine_ref = rest[3] if len(rest) > 1 else rest[0]
     for d, ref in enumerate((own_ref, p1_ref, p2_ref, p3_ref)):
 
         @pl.when(z == (k + d) % 4)
@@ -158,11 +147,12 @@
             mine_ref[...] = ref[...]
 
     if len(rest) > 1:
-        left_ref, gain_ref, _, out_ref = rest
+        left_ref, near_ref, far_ref, _, out_ref, tile_ref = rest
 
         @pl.when(z > k + 1)
         def _():
-            out_ref[...] = left_ref[...] - full_dot(mine_ref[...], gain_ref[0])
+            tile_into(place_ref, near_ref, far_ref, tile_ref)
+            out_ref[...] = left_ref[...] - dot_nt(mine_ref[...], tile_ref[...])
 
         @pl.when(z <= k + 1)
         def _():
@@ -173,31 +163,37 @@
     return pl.BlockSpec((192, 512), lambda i: (0, 0))
 
 
-def gain_spec(k):
-    return pl.BlockSpec((1, 512, 512), lambda i: (k, 0, 0))
-
-
-def step(k, place, left, gains, arrived):
+def side_specs(k):
+    return [pl.BlockSpec((4, 1, 128, 256), lambda i: (0, k, 0, 0))] * 2
+
+
+def tile_scratch():
+    return [pltpu.VMEM((512, 512), jnp.float32)]
+
+
+def step(k, place, left, sides, inverse, arrived):
     return pl.pallas_call(
         functools.partial(step_body, k),
         grid=(1,),
-        in_specs=[in_smem(), piece_spec(), gain_spec(k), piece_spec()],
+        in_specs=[in_smem(), piece_spec(), *side_specs(k), pl.BlockSpec((512, 512), lambda i: (0, 0)), piece_spec()],
         out_specs=piece_spec(),
         out_shape=f32(192, 512),
+        scratch_shapes=tile_scratch(),
         name="step",
-    )(place, left, gains, arrived)
-
-
-def late(k, place, own, arrived, left=None, gains=None):
+    )(place, left, *sides, inverse, arrived)
+
+
+def late(k, place, own, arrived, left=None, sides=None):
     more = left is not None
     return pl.pallas_call(
         functools.partial(late_body, k),
         grid=(1,),
-        in_specs=[in_smem()] + [piece_spec()] * 4 + ([piece_spec(), gain_spec(k)] if more else []),
+        in_specs=[in_smem()] + [piece_spec()] * 4 + ([piece_spec(), *side_specs(k)] if more else []),
         out_specs=[piece_spec()] * (2 if more else 1),
         out_shape=[f32(192, 512)] * (2 if more else 1),
+        scratch_shapes=tile_scratch() if more else [],
         name="late",
-    )(place, own, *arrived, *((left, gains) if more else ()))
+    )(place, own, *arrived, *((left, *sides) if more else ()))
 
 
 def pack_body(place_ref, own_ref, m1_ref, m2_ref, m3_ref, *rest):
@@ -236,52 +232,55 @@
     )(*operands)
 
 
-def update_body(halves, first, count, block_ref, into_ref, *refs):
-    xs, tiles = refs[: 2 * count], refs[2 * count : 2 * count + len(halves)]
-    out_ref, high_ref, low_ref, xh_ref, xl_ref = refs[-5:]
+def update_body(spans, place_ref, into_ref, *refs):
+    items = [(p, h, s, p - start) for s, (h, start, count) in enumerate(spans) for p in range(start, start + count)]
+    xs, tiles = refs[: 2 * len(items)], refs[2 * len(items) : 2 * len(items) + len(spans)]
+    out_ref, tile_ref, x_ref = refs[-3:]
+    depth = 256 * len(items)
 
     @pl.when(pl.program_id(0) == 0)
     def _():
-        for p in range(count):
-            for h in range(len(halves)):
-                at = (p * len(halves) + h) * 256
-                xh_ref[:, at : at + 256] = xs[2 * p][h]
-                xl_ref[:, at : at + 256] = xs[2 * p + 1][h]
-
-    block_id = block_ref[3] + pl.program_id(0) * 16
-    for p in range(count):
-        for h in range(len(halves)):
-            at = (p * len(halves) + h) * 256
-            part = jnp.where(first + p < block_id, tiles[h][p, 0], 0.0)
-            high = part.astype(jnp.bfloat16)
-            high_ref[:, at : at + 256] = high
-            low_ref[:, at : at + 256] = (part - high.astype(jnp.float32)).astype(jnp.bfloat16)
-    dims = (((1,), (1,)), ((), ()))
-    high, low = high_ref[...], low_ref[...]
-    total = lax.dot_general(xh_ref[...], high, dims, preferred_element_type=jnp.float32)
-    total += lax.dot_general(xh_ref[...], low, dims, preferred_element_type=jnp.float32)
-    total += lax.dot_general(xl_ref[...], high, dims, preferred_element_type=jnp.float32)
-    out_ref[0] = into_ref[0] - total
-
-
-def update(halves, first, place, into, xs, tiles, alias):
-    count = len(xs)
+        for i in range(len(items)):
+            high, low = xs[2 * i][0], xs[2 * i + 1][0]
+            x_ref[:, 256 * i : 256 * (i + 1)] = high
+            x_ref[:, depth + 256 * i : depth + 256 * (i + 1)] = high
+            x_ref[:, 2 * depth + 256 * i : 2 * depth + 256 * (i + 1)] = low
+
+    block_id = place_ref[3] + pl.program_id(0) * 16
+    for i, (panel, _, span, at) in enumerate(items):
+        part = jnp.where(panel < block_id, tiles[span][at, 0], 0.0)
+        high = part.astype(jnp.bfloat16)
+        tile_ref[:, 256 * i : 256 * (i + 1)] = high
+        tile_ref[:, depth + 256 * i : depth + 256 * (i + 1)] = (part - high.astype(jnp.float32)).astype(jnp.bfloat16)
+        tile_ref[:, 2 * depth + 256 * i : 2 * depth + 256 * (i + 1)] = high
+    out_ref[0] = into_ref[0] - lax.dot_general(
+        x_ref[...], tile_ref[...], (((1,), (1,)), ((), ())), preferred_element_type=jnp.float32
+    )
+
+
+def update(spans, place, into, parts, bulk, alias):
     blocks, rows, width = into.shape
     big = pl.BlockSpec((1, rows, width), lambda l: (l, 0, 0))
-    tile_spec = pl.BlockSpec((count, 1, width, 256), lambda l: (first // count, l, 0, 0))
-    x_spec = pl.BlockSpec((len(halves), rows, 256), lambda l: (halves[0], 0, 0))
-    depth = 256 * count * len(halves)
-    return pl.pallas_call(
-        functools.partial(update_body, halves, first, count),
+    operands, specs = [place, into], [in_smem(), big]
+    for h, start, count in spans:
+        for p in range(start, start + count):
+            operands += parts[p]
+            specs += [pl.BlockSpec((1, rows, 256), lambda l, h=h: (h, 0, 0))] * 2
+    for h, start, count in spans:
+        operands.append(bulk[h])
+        specs.append(pl.BlockSpec((count, 1, width, 256), lambda l, at=start // count: (at, l, 0, 0)))
+    depth = 3 * 256 * sum(count for _, _, count in spans)
+    return pl.pallas_call(
+        functools.partial(update_body, spans),
         grid=(blocks,),
-        in_specs=[in_smem(), big] + [x_spec] * (2 * count) + [tile_spec] * len(halves),
+        in_specs=specs,
         out_specs=big,
         out_shape=f32(*into.shape),
-        scratch_shapes=[pltpu.VMEM((width, depth), jnp.bfloat16)] * 2 + [pltpu.VMEM((rows, depth), jnp.bfloat16)] * 2,
+        scratch_shapes=[pltpu.VMEM((width, depth), jnp.bfloat16), pltpu.VMEM((rows, depth), jnp.bfloat16)],
         input_output_aliases={1: 0} if alias else {},
-        compiler_params=pltpu.CompilerParams(vmem_limit_bytes=48 * 1024 * 1024),
+        compiler_params=pltpu.CompilerParams(vmem_limit_bytes=52 * 1024 * 1024),
         name="update",
-    )(place, into, *[part for x in xs for part in x], *tiles)
+    )(*operands)
 
 
 def ring(shift):
@@ -289,7 +288,10 @@
 
 
 def over_z(value, k):
-    return [lax.ppermute(value, "z", [(k, (k + d) % 4)]) for d in (1, 2, 3)]
+    up = lax.ppermute(value, "z", [(k, (k + 1) % 4)])
+    down = lax.ppermute(value, "z", [(k, (k + 3) % 4)])
+    on = lax.ppermute(down, "z", [((k + 3) % 4, (k + 2) % 4)])
+    return [up, on, down]
 
 
 def over_y(value):
@@ -317,11 +319,11 @@
     tile = lax.all_gather(tile, "x")
     diag = jnp.stack(over_y(lax.dynamic_index_in_dim(tile, z, 0, keepdims=False)))
     diag_far = lax.ppermute(diag, "core", SWAP)
-    inverse, left = invert(place, rows, diag, diag_far)
+    inverse, ready = invert(place, rows, diag, diag_far)
     pieces = over_y(tile[:3])
     off = jnp.stack(pieces)
     off_far = lax.ppermute(off, "core", SWAP)
-    gains = gain(place, inverse, off, off_far)
+    sides, left = (off, off_far), rows
 
     solved, parts, before = None, [], None
 
@@ -332,22 +334,21 @@
         return solved
 
     for k in range(4):
-        sent, moved = left, over_z(left, k)
+        sent, moved = ready, over_z(ready, k)
         if k > 0:
             if k < 3:
-                mine, left = late(k - 1, place, *before, left, gains)
+                mine, left = late(k - 1, place, *before, left, sides)
             else:
                 (mine,) = late(k - 1, place, *before)
             solved = finish(k - 1, mine, solved)
         if k < 3:
-            left = step(k, place, left, gains, moved[0])
+            ready = step(k, place, left, sides, inverse, moved[0])
         before = (sent, moved)
     (mine,) = late(3, place, *before)
     solved = finish(3, mine, solved)
 
-    out = update((0,), 0, place, a, parts[:3], [near], False)
-    out = update((1,), 0, place, out, parts[:3], [far], True)
-    out = update((0, 1), 3, place, out, parts[3:], [near, far], True)
+    out = update(((0, 0, 2),), place, a, parts, (near, far), False)
+    out = update(((0, 2, 2), (1, 0, 4)), place, out, parts, (near, far), True)
     return out.transpose(1, 0, 2), solved
 
 

time: 395 us -> 388 us (0.982)
  the two profiles are of different devices: /device:TPU:1 before, /device:TPU:64 now
where the time goes in v3:
time: 388 us; the launch traced here: 387 us
  waiting for transfers between devices  197 us (51%)
  Pallas kernels  83.9 us (22%)
  starting transfers between devices  61.4 us (16%)
  between operations  14.4 us (4%)
  blocking collectives  13.1 us (3%)
  local copies, waits for them, and re-layouts  11.1 us (3%)
  other arithmetic  5.36 us (1%)
    all_gather x1, waiting for transfers between devices, placed(): near = lax.all_gather(factor, 'x')  122 us
    ppermute x18, waiting for transfers between devices, over_y(): return [value] + [lax.ppermute(value, 'y', ring(d)) for d in (1, 2, 3)]  53.2 us
    pallas_call x2, Pallas kernels, update(): pl.pallas_call(functools.partial(update_body, spans), grid=(blocks,), in_...  42.4 us
    ppermute x18, starting transfers between devices, over_y(): return [value] + [lax.ppermute(value, 'y', ring(d)) for d in (1, 2, 3)]  29.9 us
    ppermute x6, starting transfers between devices, spread(): moved = [lax.ppermute(piece(j), 'y', [(0, j)]) for j in range(1, 4)]  17 us
    pallas_call x4, Pallas kernels, pack(): pl.pallas_call(pack_body, grid=(1,), in_specs=specs, out_specs=[pl.BlockS...  13.5 us
    all_gather x1, blocking collectives, placed(): tile = lax.all_gather(tile, 'x')  13.1 us
    ppermute x4, waiting for transfers between devices, over_z(): on = lax.ppermute(down, 'z', [((k + 3) % 4, (k + 2) % 4)])  11.7 us
  transfers between devices with their start and end apart: 40, of which 19 were waited for; matrix products, arithmetic and copies ran while one was open for 3% of the time, Pallas kernels for 14%

profile of v3, /device:TPU:64, one launch (start us, length us, event | category | flops | bytes accessed | tf_op | source)
XLA Modules:
  0.0 386.6 jit_solution(2725822337058081703)
XLA Ops:
  7.9 121.9 %all-gather.4.cloned.1.call-done = f32[24,512,256]{2,1,0:T(8,128)} async-done(((f32[6,512,256]{2,1,0:T(8,128)}), f32[24,512,256]{2,1,0:T(8,128)}) %all-gather.4.cloned.1.call-update) | async-done | bytes 12582928 | tf_op jit(solution)/shard_map/all_gather | solution.py:314
  130.9 3.4 collective-permute-start.5
  134.3 2.2 collective-permute-start.4
  138.2 2.3 collective-permute-done.4
  142.2 13.1 %all-gather = f32[512,256]{1,0:T(8,128)S(1)} all-gather(f32[128,256]{1,0:T(8,128)S(1)} %fusion.4), channel_id=2, replica_groups=mesh['x'=4,'core'=2,'y'=4,'z'=4] {'x'}, dimensions={0}, use_global_device_ids=true | all-gather | bytes 655360 | tf_op jit(solution)/shard_map/all_gather | solution.py:319
  155.3 3.4 collective-permute-start.14
  159.9 2.0 collective-permute-start.15
  162.0 6.9 %collective-permute-done.14 = f32[3,128,256]{2,1,0:T(8,128)S(1)} collective-permute-done((f32[3,128,256]{2,1,0:T(8,128)S(1)}, f32[3,128,256]{2,1,0:T(8,128)S(1)}, u32[]{:S(2)}, u32[]{:S(2)}) %collective-permute-start.14) | collective-permute-done | bytes 393248 | tf_op jit(solution)/shard_map/ppermute | solution.py:298
  168.9 4.7 %collective-permute-done.13 = f32[3,128,256]{2,1,0:T(8,128)S(1)} collective-permute-done((f32[3,128,256]{2,1,0:T(8,128)S(1)}, f32[3,128,256]{2,1,0:T(8,128)S(1)}, u32[]{:S(2)}, u32[]{:S(2)}) %collective-permute-start.13) | collective-permute-done | bytes 393248 | tf_op jit(solution)/shard_map/ppermute | solution.py:298
  173.5 2.4 collective-permute-done.15
  177.9 2.5 slice_bitcast_fusion.1
  180.5 1.5 collective-permute-start.2
  182.1 2.0 collective-permute-start.6
  184.2 10.1 %collective-permute-done.7 = f32[128,256]{1,0:T(8,128)S(1)} collective-permute-done((f32[128,256]{1,0:T(8,128)S(1)}, f32[128,256]{1,0:T(8,128)S(1)}, u32[]{:S(2)}, u32[]{:S(2)}) %collective-permute-start.7) | collective-permute-done | bytes 131104 | tf_op jit(solution)/shard_map/ppermute | solution.py:298
  194.2 6.6 %collective-permute-start.1 = (f32[192,512]{1,0:T(8,128)}, f32[192,512]{1,0:T(8,128)}, u32[]{:S(2)}, u32[]{:S(2)}) collective-permute-start(f32[192,512]{1,0:T(8,128)} %get-tuple-element.39), channel_id=1, source_target_pairs={{0,8},{1,9},{2,10},{3,11},{16,24},{17,25},{18,26},{19,27},{32,40},... | collective-permute-start | bytes 1179656 | tf_op jit(solution)/shard_map/ppermute | solution.py:303
  200.8 2.1 collective-permute-start
  207.4 1.7 collective-permute-done
  209.1 1.9 fusion.2.rows_ref.rest_0_.left_ref
  211.0 7.0 %invert.1 = (f32[512,512]{1,0:T(8,128)}, f32[192,512]{1,0:T(8,128)}) custom-call(s32[4]{0:T(128)} %pad_add_fusion.place_ref, f32[192,512]{1,0:T(8,128)} %fusion.2.rows_ref.rest_0_.left_ref, f32[4,128,256]{2,1,0:T(8,128)} %pad_maximum_fusion.1.near_ref, f32[4,128,256]{2,1,0:T(8,128)} %collective-permute-done.9.far_ref), custom_call_target="tpu_custom_call" | custom-call | tf_op jit(solution)/shard_map/invert/pallas_call | solution.py:116
  222.8 2.5 step.3.own_ref
  227.3 11.7 %collective-permute-done.12.p2_ref = f32[192,512]{1,0:T(8,128)} collective-permute-done((f32[192,512]{1,0:T(8,128)}, f32[192,512]{1,0:T(8,128)}, u32[]{:S(2)}, u32[]{:S(2)}) %collective-permute-start.12) | collective-permute-done | bytes 393248 | tf_op jit(solution)/shard_map/ppermute | solution.py:293
  239.0 4.2 %late.4 = (f32[192,512]{1,0:T(8,128)}, f32[192,512]{1,0:T(8,128)}) custom-call(s32[4]{0:T(128)} %pad_add_fusion.place_ref, f32[192,512]{1,0:T(8,128)} %get-tuple-element.20.own_ref, f32[192,512]{1,0:T(8,128)} %copy-done.10, f32[192,512]{1,0:T(8,128)} %collective-permute-done.12.p2_ref, f32[192,512]{1,0:T(8,128)} %collective-permute-done.11.p3_ref, ...), custom_call_target="tpu_custom_call" | custom-call | tf_op jit(solution)/shard_map/late/pallas_call | solution.py:188
  244.0 3.3 collective-permute-done.20.p1_ref.next_ref
  248.1 4.5 %step.4.own_ref = f32[192,512]{1,0:T(8,128)} custom-call(s32[4]{0:T(128)} %pad_add_fusion.place_ref, f32[192,512]{1,0:T(8,128)} %get-tuple-element.25.rest_0_.left_ref, f32[4,3,128,256]{3,2,1,0:T(8,128)} %copy-done.5, f32[4,3,128,256]{3,2,1,0:T(8,128)} %copy-done.6, f32[512,512]{1,0:T(8,128)} %get-tuple-element.24.inverse_ref, f32[192,512]{1,0:T(8,128)} %copy-done.9), custom_call_target="tpu_custom_call" | custom-call | tf_op jit(solution)/shard_map/step/pallas_call | solution.py:175
  255.2 4.0 %collective-permute-start.19 = (f32[192,512]{1,0:T(8,128)S(1)}, f32[192,512]{1,0:T(8,128)S(1)}, u32[]{:S(2)}, u32[]{:S(2)}) collective-permute-start(f32[192,512]{1,0:T(8,128)S(1)} %copy-done.22), channel_id=1, source_target_pairs={{0,12},{4,0},{8,4},{12,8},{1,13},{5,1},{9,5},{13,9},{2,14},{6,2},{... | collective-permute-start | bytes 1179656 | tf_op jit(solution)/shard_map/ppermute | solution.py:298
  260.0 2.8 late.5
  264.4 2.5 step.5.own_ref
  268.2 3.1 collective-permute-done.19.m3_ref
  271.4 5.5 %collective-permute-start.25 = (f32[192,512]{1,0:T(8,128)S(1)}, f32[192,512]{1,0:T(8,128)S(1)}, u32[]{:S(2)}, u32[]{:S(2)}) collective-permute-start(f32[192,512]{1,0:T(8,128)S(1)} %copy-done.11), channel_id=1, source_target_pairs={{0,12},{4,0},{8,4},{12,8},{1,13},{5,1},{9,5},{13,9},{2,14},{6,2},{... | collective-permute-start | bytes 1179656 | tf_op jit(solution)/shard_map/ppermute | solution.py:298
  278.3 2.0 collective-permute-start.34
  280.4 2.2 late.6.own_ref
  283.8 1.8 collective-permute-start.23
  285.6 1.8 collective-permute-start.31
  287.4 1.5 collective-permute-start.30
  288.8 2.2 late.7.own_ref
  291.0 5.0 %collective-permute-done.24.m2_ref = f32[192,512]{1,0:T(8,128)S(1)} collective-permute-done((f32[192,512]{1,0:T(8,128)S(1)}, f32[192,512]{1,0:T(8,128)S(1)}, u32[]{:S(2)}, u32[]{:S(2)}) %collective-permute-start.24) | collective-permute-done | bytes 393248 | tf_op jit(solution)/shard_map/ppermute | solution.py:298
  296.0 2.0 collective-permute-start.29
  298.0 7.6 %collective-permute-done.23.m1_ref = f32[192,512]{1,0:T(8,128)S(1)} collective-permute-done((f32[192,512]{1,0:T(8,128)S(1)}, f32[192,512]{1,0:T(8,128)S(1)}, u32[]{:S(2)}, u32[]{:S(2)}) %collective-permute-start.23) | collective-permute-done | bytes 393248 | tf_op jit(solution)/shard_map/ppermute | solution.py:298
  307.0 6.0 %collective-permute-done.30.m2_ref = f32[192,512]{1,0:T(8,128)S(1)} collective-permute-done((f32[192,512]{1,0:T(8,128)}, f32[192,512]{1,0:T(8,128)S(1)}, u32[]{:S(2)}, u32[]{:S(2)}) %collective-permute-start.30) | collective-permute-done | bytes 393248 | tf_op jit(solution)/shard_map/ppermute | solution.py:298
  313.0 1.9 collective-permute-start.35
  314.9 3.3 pack.4
  318.2 3.3 pack.5
  323.2 3.3 pack.6
  326.5 2.7 collective-permute-done.36.m2_ref
  329.2 3.8 collective-permute-done.35.m1_ref
  333.8 3.5 pack.7
  337.3 14.1 %update.2.into_ref = f32[6,768,512]{2,1,0:T(8,128)} custom-call(s32[4]{0:T(128)S(1)} %copy-done.4, f32[6,768,512]{2,1,0:T(8,128)} %bitcast.50, bf16[2,768,256]{2,1,0:T(8,128)(2,1)S(1)} %copy-done, bf16[2,768,256]{2,1,0:T(8,128)(2,1)S(1)} %copy-done.1, bf16[2,768,256]{2,1,0:T(8,128)(2,1)} %get-tuple-element.28.refs_2_.refs_6_, ...), custom_call_target="tpu_custom_call" | custom-call | tf_op jit(solution)/shard_map/update/pallas_call | solution.py:273
  351.3 28.4 %update.3 = f32[6,768,512]{2,1,0:T(8,128)} custom-call(s32[4]{0:T(128)S(1)} %copy-done.4, f32[6,768,512]{2,1,0:T(8,128)} %update.2.into_ref, bf16[2,768,256]{2,1,0:T(8,128)(2,1)S(1)} %copy-done.2, bf16[2,768,256]{2,1,0:T(8,128)(2,1)S(1)} %copy-done.3, bf16[2,768,256]{2,1,0:T(8,128)(2,1)} %get-tuple-element.35.refs_2_.refs_10_, ...), custom_call_target="tpu_custom_call", output_to_operand_aliasing={{}: (1, {})} | custom-call | tf_op jit(solution)/shard_map/update/pallas_call | solution.py:273
  (122 shorter events, 34.0 us)
Async XLA Ops:
  7.2 122.7 %all-gather.4.cloned.1.call-start = ((), (), s32[]{:S(2)}) async-start(), calls=%async_computation | async-start | bytes 15728640 | tf_op jit(solution)/shard_map/all_gather | solution.py:314
  129.8 221.5 %collective-permute-start.38 = (f32[4,6,512,256]{3,2,1,0:T(8,128)}, f32[4,6,512,256]{3,2,1,0:T(8,128)}, u32[]{:S(2)}, u32[]{:S(2)}) collective-permute-start(f32[4,6,512,256]{3,2,1,0:T(8,128)} %bitcast.44), channel_id=1, source_target_pairs={{0,16},{16,0},{1,17},{17,1},{2,18},{18,2},{3,19},{19,3},{4,20},{20... | collective-permute-start | bytes 37748744 | tf_op jit(solution)/shard_map/ppermute | solution.py:315
  130.9 7.3 %collective-permute-start.5 = (f32[128,256]{1,0:T(8,128)S(1)}, f32[128,256]{1,0:T(8,128)S(1)}, u32[]{:S(2)}, u32[]{:S(2)}) collective-permute-start(f32[128,256]{1,0:T(8,128)S(1)} %get-tuple-element.41), channel_id=1, source_target_pairs={{0,4},{1,5},{2,6},{3,7},{16,20},{17,21},{18,22},{19,23},{32,36},{3... | collective-permute-start | bytes 393224 | tf_op jit(solution)/shard_map/ppermute | solution.py:303
  134.3 6.2 %collective-permute-start.4 = (f32[128,256]{1,0:T(8,128)S(1)}, f32[128,256]{1,0:T(8,128)S(1)}, u32[]{:S(2)}, u32[]{:S(2)}) collective-permute-start(f32[128,256]{1,0:T(8,128)S(1)} %get-tuple-element.42), channel_id=1, source_target_pairs={{0,8},{1,9},{2,10},{3,11},{16,24},{17,25},{18,26},{19,27},{32,40},... | collective-permute-start | bytes 393224 | tf_op jit(solution)/shard_map/ppermute | solution.py:303
  136.5 4.7 %collective-permute-start.3 = (f32[128,256]{1,0:T(8,128)S(1)}, f32[128,256]{1,0:T(8,128)S(1)}, u32[]{:S(2)}, u32[]{:S(2)}) collective-permute-start(f32[128,256]{1,0:T(8,128)S(1)} %get-tuple-element.43), channel_id=1, source_target_pairs={{0,12},{1,13},{2,14},{3,15},{16,28},{17,29},{18,30},{19,31},{32,44... | collective-permute-start | bytes 393224 | tf_op jit(solution)/shard_map/ppermute | solution.py:303
  155.2 21.5 %copy-start.7 = (f32[512,256]{1,0:T(8,128)}, f32[512,256]{1,0:T(8,128)S(1)}, u32[]{:S(2)}) copy-start(f32[512,256]{1,0:T(8,128)S(1)} %all-gather) | copy-start | bytes 1572868
  155.3 13.6 %collective-permute-start.14 = (f32[3,128,256]{2,1,0:T(8,128)S(1)}, f32[3,128,256]{2,1,0:T(8,128)S(1)}, u32[]{:S(2)}, u32[]{:S(2)}) collective-permute-start(f32[3,128,256]{2,1,0:T(8,128)S(1)} %bitcast.53), channel_id=1, source_target_pairs={{0,8},{4,12},{8,0},{12,4},{1,9},{5,13},{9,1},{13,5},{2,10},{6,14},... | collective-permute-start | bytes 1179656 | tf_op jit(solution)/shard_map/ppermute | solution.py:298
  158.6 14.9 %collective-permute-start.13 = (f32[3,128,256]{2,1,0:T(8,128)S(1)}, f32[3,128,256]{2,1,0:T(8,128)S(1)}, u32[]{:S(2)}, u32[]{:S(2)}) collective-permute-start(f32[3,128,256]{2,1,0:T(8,128)S(1)} %bitcast.54), channel_id=1, source_target_pairs={{0,4},{4,8},{8,12},{12,0},{1,5},{5,9},{9,13},{13,1},{2,6},{6,10},{... | collective-permute-start | bytes 1179656 | tf_op jit(solution)/shard_map/ppermute | solution.py:298
  159.9 16.1 %collective-permute-start.15 = (f32[3,128,256]{2,1,0:T(8,128)S(1)}, f32[3,128,256]{2,1,0:T(8,128)S(1)}, u32[]{:S(2)}, u32[]{:S(2)}) collective-permute-start(f32[3,128,256]{2,1,0:T(8,128)S(1)} %bitcast.55), channel_id=1, source_target_pairs={{0,12},{4,0},{8,4},{12,8},{1,13},{5,1},{9,5},{13,9},{2,14},{6,2},{... | collective-permute-start | bytes 1179656 | tf_op jit(solution)/shard_map/ppermute | solution.py:298
  161.9 20.2 %collective-permute-start.8 = (f32[128,256]{1,0:T(8,128)S(1)}, f32[128,256]{1,0:T(8,128)S(1)}, u32[]{:S(2)}, u32[]{:S(2)}) collective-permute-start(f32[128,256]{1,0:T(8,128)S(1)} %fusion.5), channel_id=1, source_target_pairs={{0,12},{4,0},{8,4},{12,8},{1,13},{5,1},{9,5},{13,9},{2,14},{6,2},{... | collective-permute-start | bytes 393224 | tf_op jit(solution)/shard_map/ppermute | solution.py:298
  177.8 40.2 %copy-start.5 = (f32[4,3,128,256]{3,2,1,0:T(8,128)}, f32[4,3,128,256]{3,2,1,0:T(8,128)S(1)}, u32[]{:S(2)}) copy-start(f32[4,3,128,256]{3,2,1,0:T(8,128)S(1)} %pad_maximum_fusion.rest_1_.near_ref) | copy-start | bytes 4718596
  177.8 43.7 %collective-permute-start.16 = (f32[4,3,128,256]{3,2,1,0:T(8,128)S(1)}, f32[4,3,128,256]{3,2,1,0:T(8,128)S(1)}, u32[]{:S(2)}, u32[]{:S(2)}) collective-permute-start(f32[4,3,128,256]{3,2,1,0:T(8,128)S(1)} %pad_maximum_fusion.rest_1_.near_ref), channel_id=1, source_target_pairs={{0,16},{16,0},{1,17},{17,1},{2,18},{18,2},{3,19},{19,3},{4,20},{20... | collective-permute-start | bytes 4718600 | tf_op jit(solution)/shard_map/ppermute | solution.py:325
  180.5 24.2 %collective-permute-start.2 = (f32[192,512]{1,0:T(8,128)S(1)}, f32[192,512]{1,0:T(8,128)S(1)}, u32[]{:S(2)}, u32[]{:S(2)}) collective-permute-start(f32[192,512]{1,0:T(8,128)S(1)} %get-tuple-element.38), channel_id=1, source_target_pairs={{0,4},{1,5},{2,6},{3,7},{16,20},{17,21},{18,22},{19,23},{32,36},{3... | collective-permute-start | bytes 1179656 | tf_op jit(solution)/shard_map/ppermute | solution.py:303
  181.9 12.3 %collective-permute-start.7 = (f32[128,256]{1,0:T(8,128)S(1)}, f32[128,256]{1,0:T(8,128)S(1)}, u32[]{:S(2)}, u32[]{:S(2)}) collective-permute-start(f32[128,256]{1,0:T(8,128)S(1)} %fusion.5), channel_id=1, source_target_pairs={{0,8},{4,12},{8,0},{12,4},{1,9},{5,13},{9,1},{13,5},{2,10},{6,14},... | collective-permute-start | bytes 393224 | tf_op jit(solution)/shard_map/ppermute | solution.py:298
  182.1 18.7 %collective-permute-start.6 = (f32[128,256]{1,0:T(8,128)S(1)}, f32[128,256]{1,0:T(8,128)S(1)}, u32[]{:S(2)}, u32[]{:S(2)}) collective-permute-start(f32[128,256]{1,0:T(8,128)S(1)} %fusion.5), channel_id=1, source_target_pairs={{0,4},{4,8},{8,12},{12,0},{1,5},{5,9},{9,13},{13,1},{2,6},{6,10},{... | collective-permute-start | bytes 393224 | tf_op jit(solution)/shard_map/ppermute | solution.py:298
  194.2 13.2 %collective-permute-start.1 = (f32[192,512]{1,0:T(8,128)}, f32[192,512]{1,0:T(8,128)}, u32[]{:S(2)}, u32[]{:S(2)}) collective-permute-start(f32[192,512]{1,0:T(8,128)} %get-tuple-element.39), channel_id=1, source_target_pairs={{0,8},{1,9},{2,10},{3,11},{16,24},{17,25},{18,26},{19,27},{32,40},... | collective-permute-start | bytes 1179656 | tf_op jit(solution)/shard_map/ppermute | solution.py:303
  200.8 8.3 %collective-permute-start = (f32[192,512]{1,0:T(8,128)S(1)}, f32[192,512]{1,0:T(8,128)}, u32[]{:S(2)}, u32[]{:S(2)}) collective-permute-start(f32[192,512]{1,0:T(8,128)S(1)} %get-tuple-element.40), channel_id=1, source_target_pairs={{0,12},{1,13},{2,14},{3,15},{16,28},{17,29},{18,30},{19,31},{32,44... | collective-permute-start | bytes 1179656 | tf_op jit(solution)/shard_map/ppermute | solution.py:303
  205.4 5.6 %collective-permute-start.9 = (f32[4,128,256]{2,1,0:T(8,128)}, f32[4,128,256]{2,1,0:T(8,128)}, u32[]{:S(2)}, u32[]{:S(2)}) collective-permute-start(f32[4,128,256]{2,1,0:T(8,128)} %pad_maximum_fusion.1.near_ref), channel_id=1, source_target_pairs={{0,16},{16,0},{1,17},{17,1},{2,18},{18,2},{3,19},{19,3},{4,20},{20... | collective-permute-start | bytes 1572872 | tf_op jit(solution)/shard_map/ppermute | solution.py:321
  218.1 2.1 collective-permute-start.11
  219.5 2.0 collective-permute-start.10
  220.2 18.8 %collective-permute-start.12 = (f32[192,512]{1,0:T(8,128)}, f32[192,512]{1,0:T(8,128)}, u32[]{:S(2)}, u32[]{:S(2)}) collective-permute-start(f32[192,512]{1,0:T(8,128)} %collective-permute-done.11.p3_ref), channel_id=1, source_target_pairs={{3,2},{7,6},{11,10},{15,14},{19,18},{23,22},{27,26},{31,30},{35,34... | collective-permute-start | bytes 1179656 | tf_op jit(solution)/shard_map/ppermute | solution.py:293
  225.3 17.8 %collective-permute-start.21 = (f32[192,512]{1,0:T(8,128)}, f32[192,512]{1,0:T(8,128)S(1)}, u32[]{:S(2)}, u32[]{:S(2)}) collective-permute-start(f32[192,512]{1,0:T(8,128)} %step.3.own_ref), channel_id=1, source_target_pairs={{1,0},{5,4},{9,8},{13,12},{17,16},{21,20},{25,24},{29,28},{33,32},... | collective-permute-start | bytes 1179656 | tf_op jit(solution)/shard_map/ppermute | solution.py:292
  226.0 21.3 %collective-permute-start.20 = (f32[192,512]{1,0:T(8,128)}, f32[192,512]{1,0:T(8,128)S(1)}, u32[]{:S(2)}, u32[]{:S(2)}) collective-permute-start(f32[192,512]{1,0:T(8,128)} %step.3.own_ref), channel_id=1, source_target_pairs={{1,2},{5,6},{9,10},{13,14},{17,18},{21,22},{25,26},{29,30},{33,34}... | collective-permute-start | bytes 1179656 | tf_op jit(solution)/shard_map/ppermute | solution.py:291
  243.1 16.1 %copy-start.30 = (f32[192,512]{1,0:T(8,128)}, f32[192,512]{1,0:T(8,128)S(1)}, u32[]{:S(2)}) copy-start(f32[192,512]{1,0:T(8,128)S(1)} %collective-permute-done.21.p3_ref) | copy-start | bytes 1179652
  243.2 16.1 %collective-permute-start.22 = (f32[192,512]{1,0:T(8,128)S(1)}, f32[192,512]{1,0:T(8,128)S(1)}, u32[]{:S(2)}, u32[]{:S(2)}) collective-permute-start(f32[192,512]{1,0:T(8,128)S(1)} %collective-permute-done.21.p3_ref), channel_id=1, source_target_pairs={{0,3},{4,7},{8,11},{12,15},{16,19},{20,23},{24,27},{28,31},{32,35}... | collective-permute-start | bytes 1179656 | tf_op jit(solution)/shard_map/ppermute | solution.py:293
  252.6 10.2 %collective-permute-start.27 = (f32[192,512]{1,0:T(8,128)}, f32[192,512]{1,0:T(8,128)S(1)}, u32[]{:S(2)}, u32[]{:S(2)}) collective-permute-start(f32[192,512]{1,0:T(8,128)} %step.4.own_ref), channel_id=1, source_target_pairs={{2,1},{6,5},{10,9},{14,13},{18,17},{22,21},{26,25},{30,29},{34,33}... | collective-permute-start | bytes 1179656 | tf_op jit(solution)/shard_map/ppermute | solution.py:292
  253.9 9.7 %collective-permute-start.26 = (f32[192,512]{1,0:T(8,128)}, f32[192,512]{1,0:T(8,128)S(1)}, u32[]{:S(2)}, u32[]{:S(2)}) collective-permute-start(f32[192,512]{1,0:T(8,128)} %step.4.own_ref), channel_id=1, source_target_pairs={{2,3},{6,7},{10,11},{14,15},{18,19},{22,23},{26,27},{30,31},{34,35... | collective-permute-start | bytes 1179656 | tf_op jit(solution)/shard_map/ppermute | solution.py:291
  255.2 16.1 %collective-permute-start.19 = (f32[192,512]{1,0:T(8,128)S(1)}, f32[192,512]{1,0:T(8,128)S(1)}, u32[]{:S(2)}, u32[]{:S(2)}) collective-permute-start(f32[192,512]{1,0:T(8,128)S(1)} %copy-done.22), channel_id=1, source_target_pairs={{0,12},{4,0},{8,4},{12,8},{1,13},{5,1},{9,5},{13,9},{2,14},{6,2},{... | collective-permute-start | bytes 1179656 | tf_op jit(solution)/shard_map/ppermute | solution.py:298
  259.2 12.1 %collective-permute-start.18 = (f32[192,512]{1,0:T(8,128)S(1)}, f32[192,512]{1,0:T(8,128)S(1)}, u32[]{:S(2)}, u32[]{:S(2)}) collective-permute-start(f32[192,512]{1,0:T(8,128)S(1)} %copy-done.22), channel_id=1, source_target_pairs={{0,8},{4,12},{8,0},{12,4},{1,9},{5,13},{9,1},{13,5},{2,10},{6,14},... | collective-permute-start | bytes 1179656 | tf_op jit(solution)/shard_map/ppermute | solution.py:298
  262.8 17.6 %copy-start.26 = (f32[192,512]{1,0:T(8,128)}, f32[192,512]{1,0:T(8,128)S(1)}, u32[]{:S(2)}) copy-start(f32[192,512]{1,0:T(8,128)S(1)} %collective-permute-done.27.p3_ref) | copy-start | bytes 1179652
  262.8 14.1 %collective-permute-start.28 = (f32[192,512]{1,0:T(8,128)S(1)}, f32[192,512]{1,0:T(8,128)S(1)}, u32[]{:S(2)}, u32[]{:S(2)}) collective-permute-start(f32[192,512]{1,0:T(8,128)S(1)} %collective-permute-done.27.p3_ref), channel_id=1, source_target_pairs={{1,0},{5,4},{9,8},{13,12},{17,16},{21,20},{25,24},{29,28},{33,32},... | collective-permute-start | bytes 1179656 | tf_op jit(solution)/shard_map/ppermute | solution.py:293
  266.9 11.4 %collective-permute-start.33 = (f32[192,512]{1,0:T(8,128)}, f32[192,512]{1,0:T(8,128)S(1)}, u32[]{:S(2)}, u32[]{:S(2)}) collective-permute-start(f32[192,512]{1,0:T(8,128)} %step.5.own_ref), channel_id=1, source_target_pairs={{3,2},{7,6},{11,10},{15,14},{19,18},{23,22},{27,26},{31,30},{35,34... | collective-permute-start | bytes 1179656 | tf_op jit(solution)/shard_map/ppermute | solution.py:292
  271.4 14.2 %copy-start.23 = (f32[192,512]{1,0:T(8,128)}, f32[192,512]{1,0:T(8,128)S(1)}, u32[]{:S(2)}) copy-start(f32[192,512]{1,0:T(8,128)S(1)} %collective-permute-done.19.m3_ref) | copy-start | bytes 1179652
  271.4 11.2 %collective-permute-start.17 = (f32[192,512]{1,0:T(8,128)S(1)}, f32[192,512]{1,0:T(8,128)S(1)}, u32[]{:S(2)}, u32[]{:S(2)}) collective-permute-start(f32[192,512]{1,0:T(8,128)S(1)} %copy-done.22), channel_id=1, source_target_pairs={{0,4},{4,8},{8,12},{12,0},{1,5},{5,9},{9,13},{13,1},{2,6},{6,10},{... | collective-permute-start | bytes 1179656 | tf_op jit(solution)/shard_map/ppermute | solution.py:298
  271.4 12.4 %collective-permute-start.25 = (f32[192,512]{1,0:T(8,128)S(1)}, f32[192,512]{1,0:T(8,128)S(1)}, u32[]{:S(2)}, u32[]{:S(2)}) collective-permute-start(f32[192,512]{1,0:T(8,128)S(1)} %copy-done.11), channel_id=1, source_target_pairs={{0,12},{4,0},{8,4},{12,8},{1,13},{5,1},{9,5},{13,9},{2,14},{6,2},{... | collective-permute-start | bytes 1179656 | tf_op jit(solution)/shard_map/ppermute | solution.py:298
  276.9 8.7 %collective-permute-start.32 = (f32[192,512]{1,0:T(8,128)}, f32[192,512]{1,0:T(8,128)}, u32[]{:S(2)}, u32[]{:S(2)}) collective-permute-start(f32[192,512]{1,0:T(8,128)} %step.5.own_ref), channel_id=1, source_target_pairs={{3,0},{7,4},{11,8},{15,12},{19,16},{23,20},{27,24},{31,28},{35,32}... | collective-permute-start | bytes 1179656 | tf_op jit(solution)/shard_map/ppermute | solution.py:291
  278.3 9.0 %collective-permute-start.34 = (f32[192,512]{1,0:T(8,128)S(1)}, f32[192,512]{1,0:T(8,128)}, u32[]{:S(2)}, u32[]{:S(2)}) collective-permute-start(f32[192,512]{1,0:T(8,128)S(1)} %collective-permute-done.33.p3_ref), channel_id=1, source_target_pairs={{2,1},{6,5},{10,9},{14,13},{18,17},{22,21},{26,25},{30,29},{34,33}... | collective-permute-start | bytes 1179656 | tf_op jit(solution)/shard_map/ppermute | solution.py:293
  282.5 13.5 %collective-permute-start.24 = (f32[192,512]{1,0:T(8,128)S(1)}, f32[192,512]{1,0:T(8,128)S(1)}, u32[]{:S(2)}, u32[]{:S(2)}) collective-permute-start(f32[192,512]{1,0:T(8,128)S(1)} %copy-done.11), channel_id=1, source_target_pairs={{0,8},{4,12},{8,0},{12,4},{1,9},{5,13},{9,1},{13,5},{2,10},{6,14},... | collective-permute-start | bytes 1179656 | tf_op jit(solution)/shard_map/ppermute | solution.py:298
  283.8 34.5 %copy-start.12 = (f32[192,512]{1,0:T(8,128)}, f32[192,512]{1,0:T(8,128)S(1)}, u32[]{:S(2)}) copy-start(f32[192,512]{1,0:T(8,128)S(1)} %collective-permute-done.25.m3_ref) | copy-start | bytes 1179652
  283.8 21.9 %collective-permute-start.23 = (f32[192,512]{1,0:T(8,128)S(1)}, f32[192,512]{1,0:T(8,128)S(1)}, u32[]{:S(2)}, u32[]{:S(2)}) collective-permute-start(f32[192,512]{1,0:T(8,128)S(1)} %copy-done.11), channel_id=1, source_target_pairs={{0,4},{4,8},{8,12},{12,0},{1,5},{5,9},{9,13},{13,1},{2,6},{6,10},{... | collective-permute-start | bytes 1179656 | tf_op jit(solution)/shard_map/ppermute | solution.py:298
  285.6 20.1 %collective-permute-start.31 = (f32[192,512]{1,0:T(8,128)}, f32[192,512]{1,0:T(8,128)S(1)}, u32[]{:S(2)}, u32[]{:S(2)}) collective-permute-start(f32[192,512]{1,0:T(8,128)} %late.6.own_ref), channel_id=1, source_target_pairs={{0,12},{4,0},{8,4},{12,8},{1,13},{5,1},{9,5},{13,9},{2,14},{6,2},{... | collective-permute-start | bytes 1179656 | tf_op jit(solution)/shard_map/ppermute | solution.py:298
  287.4 25.6 %collective-permute-start.30 = (f32[192,512]{1,0:T(8,128)}, f32[192,512]{1,0:T(8,128)S(1)}, u32[]{:S(2)}, u32[]{:S(2)}) collective-permute-start(f32[192,512]{1,0:T(8,128)} %late.6.own_ref), channel_id=1, source_target_pairs={{0,8},{4,12},{8,0},{12,4},{1,9},{5,13},{9,1},{13,5},{2,10},{6,14},... | collective-permute-start | bytes 1179656 | tf_op jit(solution)/shard_map/ppermute | solution.py:298
  296.0 22.2 %copy-start.13 = (f32[192,512]{1,0:T(8,128)}, f32[192,512]{1,0:T(8,128)S(1)}, u32[]{:S(2)}) copy-start(f32[192,512]{1,0:T(8,128)S(1)} %collective-permute-done.24.m2_ref) | copy-start | bytes 1179652
  296.0 26.4 %collective-permute-start.29 = (f32[192,512]{1,0:T(8,128)}, f32[192,512]{1,0:T(8,128)S(1)}, u32[]{:S(2)}, u32[]{:S(2)}) collective-permute-start(f32[192,512]{1,0:T(8,128)} %late.6.own_ref), channel_id=1, source_target_pairs={{0,4},{4,8},{8,12},{12,0},{1,5},{5,9},{9,13},{13,1},{2,6},{6,10},{... | collective-permute-start | bytes 1179656 | tf_op jit(solution)/shard_map/ppermute | solution.py:298
  305.6 20.9 %collective-permute-start.37 = (f32[192,512]{1,0:T(8,128)}, f32[192,512]{1,0:T(8,128)S(1)}, u32[]{:S(2)}, u32[]{:S(2)}) collective-permute-start(f32[192,512]{1,0:T(8,128)} %late.7.own_ref), channel_id=1, source_target_pairs={{0,12},{4,0},{8,4},{12,8},{1,13},{5,1},{9,5},{13,9},{2,14},{6,2},{... | collective-permute-start | bytes 1179656 | tf_op jit(solution)/shard_map/ppermute | solution.py:298
  305.7 15.9 %copy-start.14 = (f32[192,512]{1,0:T(8,128)}, f32[192,512]{1,0:T(8,128)S(1)}, u32[]{:S(2)}) copy-start(f32[192,512]{1,0:T(8,128)S(1)} %collective-permute-done.31.m3_ref) | copy-start | bytes 1179652
  305.7 23.5 %collective-permute-start.36 = (f32[192,512]{1,0:T(8,128)}, f32[192,512]{1,0:T(8,128)S(1)}, u32[]{:S(2)}, u32[]{:S(2)}) collective-permute-start(f32[192,512]{1,0:T(8,128)} %late.7.own_ref), channel_id=1, source_target_pairs={{0,8},{4,12},{8,0},{12,4},{1,9},{5,13},{9,1},{13,5},{2,10},{6,14},... | collective-permute-start | bytes 1179656 | tf_op jit(solution)/shard_map/ppermute | solution.py:298
  313.0 20.0 %collective-permute-start.35 = (f32[192,512]{1,0:T(8,128)}, f32[192,512]{1,0:T(8,128)S(1)}, u32[]{:S(2)}, u32[]{:S(2)}) collective-permute-start(f32[192,512]{1,0:T(8,128)} %late.7.own_ref), channel_id=1, source_target_pairs={{0,4},{4,8},{8,12},{12,0},{1,5},{5,9},{9,13},{13,1},{2,6},{6,10},{... | collective-permute-start | bytes 1179656 | tf_op jit(solution)/shard_map/ppermute | solution.py:298
  (24 other events, 130.7 us)
Sparse Core Ops, SparseCore 0:
  9.6 120.1 all-gather.3
